TPU v7x, 16 devices: a whole 2x2x2 slice. The times are simulated.
16 devices in a mesh: dp: 4 (over z, y), tp: 4 (over x, core).
Axes of the slice: x: 2, y: 2, z: 2, core: 2. Of those that a mesh axis runs over, the one named last changes fastest.
Arguments:
- hidden: bfloat16 [64, 5, 5120], P('dp'), parts along dimension 0
- draft_ids: int32 [64, 4], P('dp'), parts along dimension 0
- norm_gain: bfloat16 [5120], replicated
- head_w: bfloat16 [5120, 32000], P(None, 'tp')
Outputs:
- output 1: float32 [64, 4], P('dp'), parts along dimension 0
- output 2: float32 [64, 5], P('dp'), parts along dimension 0
- output 3: float32 [64, 5], P('dp'), parts along dimension 0
There are 4 independent parts. A program takes and returns all parts, laid end to end along the dimension named above; an argument that names none is the same for every part.
All inputs are finite; a program needn't handle non-finite values.
Results may differ from a plain program's by a relative error of at most 0.001.
Values sent between devices are 32-bit elements.
A program may use at most 1 GiB of HBM per device.

v0:
```python
import jax
import jax.numpy as jnp
from jax import lax
from jax.sharding import PartitionSpec as P

NORM_EPS = 1e-5


def rms_norm(hidden, norm_gain):
    wide_x = hidden.astype(jnp.float32)
    inv_rms = lax.rsqrt(jnp.mean(wide_x * wide_x, axis=-1, keepdims=True) + NORM_EPS)
    return (wide_x * inv_rms * norm_gain.astype(jnp.float32)).astype(jnp.bfloat16)


def solution(mesh):
    def per_device(hidden, draft_ids, norm_gain, head_w):
        normed = rms_norm(hidden, norm_gain)
        logits = jnp.einsum('btd,dv->btv', normed, head_w, preferred_element_type=jnp.float32)
        gathered = lax.all_gather(logits, 'tp')
        shards = gathered.shape[0]
        shard_cols = gathered.shape[3]
        drafts = draft_ids.shape[1]
        row_max = jnp.max(gathered, axis=(0, 3))
        shifted = gathered - row_max[None, :, :, None]
        exp_vals = jnp.exp(shifted)
        exp_sum = jnp.sum(exp_vals, axis=(0, 3))
        weighted = jnp.sum(exp_vals * shifted, axis=(0, 3))
        log_sum = jnp.log(exp_sum)
        log_norm = row_max + log_sum
        entropy = log_sum - weighted / exp_sum
        col_ids = lax.broadcasted_iota(jnp.int32, (shards, 1, 1, shard_cols), 0) * shard_cols + lax.broadcasted_iota(jnp.int32, (shards, 1, 1, shard_cols), 3)
        picked = jnp.sum(jnp.where(col_ids == draft_ids[None, :, :, None], gathered[:, :, :drafts], 0.0), axis=(0, 3))
        return picked - log_norm[:, :drafts], log_norm, entropy

    specs_in = (P('dp', None, None), P('dp', None), P(None), P(None, 'tp'))
    specs_out = (P('dp', None), P('dp', None), P('dp', None))
    return jax.shard_map(per_device, mesh=mesh, in_specs=specs_in, out_specs=specs_out, check_vma=False)
```

profile of v0, /device:TPU:0, one launch (start us, length us, event | category | flops | bytes accessed | tf_op | source)
XLA Modules:
  0.0 136.7 jit_solution(16982613085782469570)
XLA Ops:
  7.2 0.0 all-gather.3.cloned.1.call-start
  7.2 0.7 convert_element_type.10
  7.9 1.4 %fusion.4 = f32[16,5]{0,1:T(8,128)S(1)} fusion(bf16[16,5,5120]{2,0,1:T(8,128)(2,1)} %param.4), kind=kLoop, calls=%fused_computation.9 | loop fusion | flops 1228720 | bytes 819520 | tf_op jit(solution)/shard_map/reduce_sum | solution.py:11
  9.3 34.6 %fusion = f32[16,5,8000]{2,0,1:T(8,128)} fusion(bf16[5120,8000]{0,1:T(8,128)(2,1)} %param.7, bf16[16,5,5120]{2,0,1:T(8,128)(2,1)} %param.4, f32[5120]{0:T(1024)S(1)} %convert_element_type.10, f32[16,5]{0,1:T(8,128)S(1)} %add_rsqrt_fusion), kind=kOutput, calls=%fused_computation | convolution fusion | flops 6555238400 | bytes 85320000 | tf_op jit(solution)/shard_map/btd,dv->btv/dot_general | solution.py:18
  43.9 0.0 all-gather.3.cloned.1.call-update
  43.9 0.1 iota_add_fusion
  44.0 0.0 copy-start.2
  44.0 70.7 %all-gather.3.cloned.1.call-done = f32[64,5,8000]{2,0,1:T(8,128)} async-done(((f32[16,5,8000]{2,0,1:T(8,128)}), f32[64,5,8000]{2,0,1:T(8,128)}) %all-gather.3.cloned.1.call-update) | async-done | bytes 10240016 | tf_op jit(solution)/shard_map/all_gather | solution.py:19
  114.7 4.5 %reduce = f32[64,5]{0,1:T(8,128)S(1)} reduce(f32[64,5,8000]{2,0,1:T(8,128)} %all-gather.3.cloned.1.call-done, f32[]{:T(128)} %constant.10.clone.1), dimensions={2}, to_apply=%region_2.0 | reduce | flops 2559680 | bytes 10241284 | tf_op jit(solution)/shard_map/reduce_max | solution.py:23
  119.2 0.1 reshape.32
  119.3 0.0 copy-start
  119.3 7.9 %fusion.2 = (f32[16,5]{0,1:T(8,128)S(1)}, f32[16,5]{0,1:T(8,128)S(1)}) fusion(f32[4,16,5,8000]{3,1,0,2:T(8,128)} %bitcast.6, f32[16,5]{0,1:T(8,128)S(1)} %reduce_max.9), kind=kLoop, calls=%fused_computation.4 | loop fusion | flops 10239840 | bytes 10240960 | tf_op jit(solution)/shard_map/reduce_sum | solution.py:27
  127.1 0.6 divide_subtract_fusion
  127.7 0.0 copy-done.2
  127.8 0.0 copy-done
  127.8 0.0 copy-start.1
  127.8 1.5 %fusion.3 = f32[16,4]{0,1:T(4,128)S(1)} fusion(f32[4,16,5,8000]{3,1,0,2:T(8,128)S(1)} %bitcast.7, s32[16,4]{0,1:T(4,128)S(1)} %copy-done.2, s32[4,8000]{1,0:T(4,128)S(1)} %iota_add_fusion), kind=kLoop, calls=%fused_computation.6 | loop fusion | flops 6143936 | bytes 8320512 | tf_op jit(solution)/shard_map/reduce_sum | solution.py:32
  129.3 0.6 slice_subtract_fusion
  129.9 0.0 copy-done.1
  (3 shorter events, 0.0 us)
Async XLA Ops:
  7.2 107.5 %all-gather.3.cloned.1.call-start = ((), (), s32[]{:S(2)}) async-start(), calls=%async_computation | async-start | bytes 12902400 | tf_op jit(solution)/shard_map/all_gather | solution.py:19
  44.0 83.8 %copy-start.2 = (s32[16,4]{0,1:T(4,128)S(1)}, s32[16,4]{0,1:T(4,128)}, u32[]{:S(2)}) copy-start(s32[16,4]{0,1:T(4,128)} %param.5) | copy-start | bytes 772
  119.3 8.5 %copy-start = (f32[64,5,8000]{2,0,1:T(8,128)S(1)}, f32[64,5,8000]{2,0,1:T(8,128)}, u32[]{:S(2)}) copy-start(f32[64,5,8000]{2,0,1:T(8,128)} %all-gather.3.cloned.1.call-done) | copy-start | bytes 30720004
  127.8 2.1 %copy-start.1 = (f32[16,5]{0,1:T(8,128)}, f32[16,5]{0,1:T(8,128)S(1)}, u32[]{:S(2)}) copy-start(f32[16,5]{0,1:T(8,128)S(1)} %get-tuple-element.6) | copy-start | bytes 964
Sparse Core Ops, SparseCore 0:
  44.0 70.6 all-gather.2
where the time goes:
time: 137 us
  waiting for transfers between devices  70.7 us (52%)
  matrix products  34.6 us (25%)
  other arithmetic  17.3 us (13%)
  between operations  14.1 us (10%)
    all_gather x1, waiting for transfers between devices, per_device(): gathered = lax.all_gather(logits, 'tp')  70.7 us
    dot_general x1, matrix products, per_device(): jnp.einsum('btd,dv->btv', normed, head_w, preferred_element_type=jnp.floa...  34.6 us
    reduce_sum x1, other arithmetic, per_device(): weighted = jnp.sum(exp_vals * shifted, axis=(0, 3))  7.86 us
    reduce_max x2, other arithmetic, per_device(): row_max = jnp.max(gathered, axis=(0, 3))  4.52 us
  transfers between devices with their start and end apart: 1, of which 1 were waited for; matrix products, arithmetic and copies ran while one was open for 0% of the time, Pallas kernels for 0%

commit v1 on v0

v1 whole, which is shorter than its diff:
```python
import jax
import jax.numpy as jnp
from jax import lax
from jax.experimental import pallas as pl
from jax.experimental.pallas import tpu as pltpu
from jax.sharding import PartitionSpec as P

NORM_EPS = 1e-5
MESH = pl.DeviceIdType.MESH
LANES = 128
SLOTS = 8
CHUNK = 400


def rows_sum(block):
    return jnp.sum(block.reshape(-1, 8, block.shape[-1]), axis=0)


def rows_max(block):
    return jnp.max(block.reshape(-1, 8, block.shape[-1]), axis=0)


def update_stats(first, z, row_ids, ids, carry):
    m, s, w, p = carry
    bm = rows_max(z)
    m = jnp.where(first, bm, m)
    mn = jnp.maximum(m, bm)
    dm = m - mn
    a = jnp.exp(dm)
    z3 = z.reshape(-1, 8, z.shape[-1])
    sh = z3 - mn[None]
    e = jnp.exp(sh)
    w = a * (w + dm * s) + jnp.sum(e * sh, axis=0)
    s = a * s + jnp.sum(e, axis=0)
    p = p + rows_sum(jnp.where(row_ids == ids, z, 0.0))
    return mn, s, w, p


def pack_stats(carry):
    m, s, w, p = carry
    top = jnp.max(m, axis=0, keepdims=True)
    dm = m - top
    f = jnp.exp(dm)
    return (
        top,
        jnp.sum(f * s, axis=0, keepdims=True),
        jnp.sum(f * (w + dm * s), axis=0, keepdims=True),
        jnp.sum(p, axis=0, keepdims=True),
    )


def solution(mesh):
    tp = mesh.shape['tp']

    def per_device(hidden, draft_ids, norm_gain, head_w):
        batch, pos, dim = hidden.shape
        drafts = draft_ids.shape[1]
        cols = head_w.shape[1]
        rows = batch * pos
        kblocks = dim // LANES
        chunks = cols // CHUNK

        def kernel(x_hbm, ids_hbm, g_hbm, w_hbm, o_logp, o_logn, o_ent,
                   wv, xv, nb, gv, gf, idv, sq, st, rs, wsem, lsem, ssem, rsem):
            t = lax.axis_index('tp')
            d = lax.axis_index('dp')
            cx = pltpu.make_async_copy(x_hbm, xv, lsem.at[0])
            cg = pltpu.make_async_copy(g_hbm, gv, lsem.at[1])
            ci = pltpu.make_async_copy(ids_hbm, idv, lsem.at[2])
            cx.start()
            cg.start()
            ci.start()

            def w_copy(j, slot):
                return pltpu.make_async_copy(
                    w_hbm.at[pl.ds(pl.multiple_of(j * CHUNK, CHUNK), CHUNK), :], wv.at[slot], wsem.at[slot])

            for j in range(SLOTS):
                w_copy(j, j).start()
            barrier = pltpu.get_barrier_semaphore()
            for k in range(1, tp):
                pl.semaphore_signal(barrier, inc=1, device_id=(d, lax.rem(t + k, tp)), device_id_type=MESH)
            nb[rows:, :] = jnp.zeros((LANES - rows, dim), jnp.bfloat16)
            cg.wait()
            gf[...] = gv[...].astype(jnp.float32)
            ci.wait()
            ids = jnp.concatenate([idv[k:k + 1, :] for k in range(drafts)]
                                  + [jnp.full((1, LANES - drafts * batch), -1, jnp.int32)], axis=1)
            ids = ids - t * cols
            cx.wait()
            acc = jnp.zeros((rows, LANES), jnp.float32)
            for k in range(kblocks):
                x = xv[:, k * LANES:(k + 1) * LANES].astype(jnp.float32)
                acc = acc + x * x
            inv = lax.rsqrt(jnp.sum(acc, axis=1, keepdims=True) / dim + NORM_EPS)
            for k in range(kblocks):
                x = xv[:, k * LANES:(k + 1) * LANES].astype(jnp.float32)
                nb[:rows, k * LANES:(k + 1) * LANES] = (x * inv * gf[k:k + 1, :]).astype(jnp.bfloat16)

            row_iota = lax.broadcasted_iota(jnp.int32, (CHUNK, LANES), 0)

            def step(j, carry):
                slot = lax.rem(j, SLOTS)
                w_copy(j, slot).wait()
                z = lax.dot_general(wv[slot], nb[...], (((1,), (1,)), ((), ())), preferred_element_type=jnp.float32)

                @pl.when(j + SLOTS < chunks)
                def _():
                    w_copy(j + SLOTS, slot).start()

                return update_stats(j == 0, z, row_iota, ids - j * CHUNK, carry)

            zero = jnp.zeros((8, LANES), jnp.float32)
            carry = lax.fori_loop(0, chunks, step, (zero, zero, zero, zero))
            packed = pack_stats(carry)
            for k in range(4):
                st[k:k + 1, :] = packed[k]
                rs[t, k:k + 1, :] = packed[k]
            pl.semaphore_wait(barrier, tp - 1)
            sends = []
            for k in range(1, tp):
                peer = lax.rem(t + k, tp)
                c = pltpu.make_async_remote_copy(
                    src_ref=st, dst_ref=rs.at[t], send_sem=ssem.at[k], recv_sem=rsem.at[t],
                    device_id=(d, peer), device_id_type=MESH)
                c.start()
                sends.append(c)
            for k in range(1, tp):
                peer = lax.rem(t + k, tp)
                pltpu.make_async_remote_copy(
                    src_ref=st, dst_ref=rs.at[peer], send_sem=ssem.at[k], recv_sem=rsem.at[peer],
                    device_id=(d, peer), device_id_type=MESH).wait_recv()
            ms = [rs[k, 0:1, :] for k in range(tp)]
            top = ms[0]
            for k in range(1, tp):
                top = jnp.maximum(top, ms[k])
            s = jnp.zeros((1, LANES), jnp.float32)
            w = s
            p = s
            for k in range(tp):
                dm = ms[k] - top
                f = jnp.exp(dm)
                s = s + f * rs[k, 1:2, :]
                w = w + f * (rs[k, 2:3, :] + dm * rs[k, 1:2, :])
                p = p + rs[k, 3:4, :]
            log_sum = jnp.log(s)
            log_norm = top + log_sum
            ent = log_sum - w / s
            logp = p - log_norm
            for k in range(pos):
                o_logn[k:k + 1, :] = log_norm[:, k * batch:(k + 1) * batch]
                o_ent[k:k + 1, :] = ent[:, k * batch:(k + 1) * batch]
            for k in range(drafts):
                o_logp[k:k + 1, :] = logp[:, k * batch:(k + 1) * batch]
            for c in sends:
                c.wait_send()

        hbm = pl.BlockSpec(memory_space=pl.ANY)
        vmem = pl.BlockSpec(memory_space=pltpu.VMEM)
        f32 = jnp.float32
        logp, logn, ent = pl.pallas_call(
            kernel,
            out_shape=[jax.ShapeDtypeStruct((drafts, batch), f32), jax.ShapeDtypeStruct((pos, batch), f32),
                       jax.ShapeDtypeStruct((pos, batch), f32)],
            in_specs=[hbm] * 4,
            out_specs=[vmem] * 3,
            scratch_shapes=[
                pltpu.VMEM((SLOTS, CHUNK, dim), jnp.bfloat16),
                pltpu.VMEM((rows, dim), jnp.bfloat16),
                pltpu.VMEM((LANES, dim), jnp.bfloat16),
                pltpu.VMEM((kblocks, LANES), jnp.bfloat16),
                pltpu.VMEM((kblocks, LANES), f32),
                pltpu.VMEM((drafts, batch), jnp.int32),
                pltpu.VMEM((8, LANES), f32),
                pltpu.VMEM((8, LANES), f32),
                pltpu.VMEM((tp, 8, LANES), f32),
                pltpu.SemaphoreType.DMA((SLOTS,)),
                pltpu.SemaphoreType.DMA((3,)),
                pltpu.SemaphoreType.DMA((tp,)),
                pltpu.SemaphoreType.DMA((tp,)),
            ],
            compiler_params=pltpu.CompilerParams(
                collective_id=0, has_side_effects=True, vmem_limit_bytes=60 * 1024 * 1024),
        )(hidden.transpose(1, 0, 2).reshape(rows, dim), draft_ids.T, norm_gain.reshape(kblocks, LANES), head_w.T)
        return logp.T, logn.T, ent.T

    specs_in = (P('dp', None, None), P('dp', None), P(None), P(None, 'tp'))
    specs_out = (P('dp', None), P('dp', None), P('dp', None))
    return jax.shard_map(per_device, mesh=mesh, in_specs=specs_in, out_specs=specs_out, check_vma=False)
```

time: 137 us -> 45.7 us (0.33)
  waiting for transfers between devices: 70.7 us -> 0 us
  Pallas kernels: 0 us -> 41.1 us
  matrix products: 34.6 us -> 0 us
  other arithmetic: 17.3 us -> 0 us
  between operations: 14.1 us -> 0.64 us
  local copies, waits for them, and re-layouts: 0.09 us -> 3.77 us
    all_gather x1 -> x0, waiting for transfers between devices: 70.7 us -> none  [per_device(): gathered = lax.all_gather(logits, 'tp')]
    pallas_call x0 -> x1, Pallas kernels: none -> 41.1 us  [per_device(): pl.pallas_call(kernel, out_shape=[jax.ShapeDtypeStruct((drafts, batch), f...]
    dot_general x1 -> x0, matrix products: 34.6 us -> none  [per_device(): jnp.einsum('btd,dv->btv', normed, head_w, preferred_element_type=jnp.floa...]
    reduce_sum x3 -> x0, other arithmetic: 10.8 us -> none  [the longest x1 7.86 us: per_device(): weighted = jnp.sum(exp_vals * shifted, axis=(0, 3))]
    reduce_max x2 -> x0, other arithmetic: 4.52 us -> none  [per_device(): row_max = jnp.max(gathered, axis=(0, 3))]
    unnamed x6 -> x3, local copies, waits for them, and re-layouts: 0.01 us -> 3.77 us
  transfers between devices with their start and end apart: 1 -> 0, of which waited for: 1 -> 0; matrix products, arithmetic and copies ran while one was open for 0% -> 0% of each run, Pallas kernels for 0% -> 0%
where the time goes in v1:
time: 45.7 us; the launch traced here: 45.5 us
  Pallas kernels  41.1 us (90%)
  local copies, waits for them, and re-layouts  3.77 us (8%)
  between operations  0.64 us (1%)
    pallas_call x1, Pallas kernels, per_device(): pl.pallas_call(kernel, out_shape=[jax.ShapeDtypeStruct((drafts, batch), f...  41.1 us
    unnamed x3, local copies, waits for them, and re-layouts  3.77 us

profile of v1, /device:TPU:0, one launch (start us, length us, event | category | flops | bytes accessed | tf_op | source)
XLA Modules:
  0.0 45.5 jit_solution(9388081243463925953)
XLA Ops:
  0.6 41.1 %shard_map.67 = (f32[4,16]{1,0:T(4,128)}, f32[5,16]{1,0:T(8,128)}, f32[5,16]{1,0:T(8,128)}) custom-call(bf16[80,5120]{1,0:T(8,128)(2,1)} %bitcast.9, s32[4,16]{1,0:T(4,128)} %bitcast.13, bf16[40,128]{1,0:T(8,128)(2,1)} %bitcast.10, bf16[8000,5120]{1,0:T(8,128)(2,1)} %bitcast.4.w_hbm), custom_call_target="tpu_custom_call" | custom-call | tf_op jit(solution)/shard_map/pallas_call | solution.py:161
  41.8 1.2 %copy.10 = f32[16,4]{0,1:T(4,128)} copy(f32[16,4]{0,1:T(4,128)} %bitcast.14) | data formatting | bytes 512
  43.0 1.3 %copy.11 = f32[16,5]{0,1:T(8,128)} copy(f32[16,5]{0,1:T(8,128)} %bitcast.12) | data formatting | bytes 640
  44.3 1.3 %copy.12 = f32[16,5]{0,1:T(8,128)} copy(f32[16,5]{0,1:T(8,128)} %bitcast.11) | data formatting | bytes 640

commit v2 on v1

v2 whole, which is shorter than its diff:
```python
import jax
import jax.numpy as jnp
from jax import lax
from jax.experimental import pallas as pl
from jax.experimental.pallas import tpu as pltpu
from jax.sharding import PartitionSpec as P

NORM_EPS = 1e-5
MESH = pl.DeviceIdType.MESH
LANES = 128
TILE = 256
BLOCK = 800
NT = (((1,), (1,)), ((), ()))


def rows_sum(block):
    return jnp.sum(block.reshape(-1, 8, block.shape[-1]), axis=0)


def rows_max(block):
    return jnp.max(block.reshape(-1, 8, block.shape[-1]), axis=0)


def update_stats(z, row_ids, ids, carry):
    bm = rows_max(z)
    z3 = z.reshape(-1, 8, z.shape[-1])
    picked = rows_sum(jnp.where(row_ids == ids, z, 0.0))
    if carry is None:
        sh = z3 - bm[None]
        e = jnp.exp(sh)
        return bm, jnp.sum(e, axis=0), jnp.sum(e * sh, axis=0), picked
    m, s, w, p = carry
    mn = jnp.maximum(m, bm)
    dm = m - mn
    a = jnp.exp(dm)
    sh = z3 - mn[None]
    e = jnp.exp(sh)
    w = a * (w + dm * s) + jnp.sum(e * sh, axis=0)
    s = a * s + jnp.sum(e, axis=0)
    return mn, s, w, p + picked


def pack_stats(carry):
    m, s, w, p = carry
    top = jnp.max(m, axis=0, keepdims=True)
    dm = m - top
    f = jnp.exp(dm)
    return (
        top,
        jnp.sum(f * s, axis=0, keepdims=True),
        jnp.sum(f * (w + dm * s), axis=0, keepdims=True),
        jnp.sum(p, axis=0, keepdims=True),
    )


def solution(mesh):
    tp = mesh.shape['tp']

    def per_device(hidden, draft_ids, norm_gain, head_w):
        batch, pos, dim = hidden.shape
        drafts = draft_ids.shape[1]
        cols = head_w.shape[1]
        half = cols // 2
        rows = batch * pos
        kblocks = dim // LANES
        tiles = dim // TILE
        parts = kblocks // tp
        ptiles = tiles // tp
        nblocks = half // BLOCK
        f32 = jnp.float32

        def kernel(x_hbm, ids_hbm, g_hbm, w_hbm, o_logp, o_logn, o_ent,
                   wv, xv, nb, nf, pf, acc, gv, gf, idv, idp, st, rs,
                   wsem, lsem, ysend, yrecv, xsend, xrecv, asend, arecv, bsend, brecv, isend, irecv, ssem, rsem):
            t = lax.axis_index('tp')
            d = lax.axis_index('dp')
            y = lax.rem(d, 2)
            core = lax.rem(t, 2)
            mate = (d + 1 - 2 * y, t)
            sib = (d, t + 1 - 2 * core)
            nbr_t = lax.rem(t + 2, tp)
            nbr = (d, nbr_t)
            sib_t = t + 1 - 2 * core
            far_t = lax.rem(sib_t + 2, tp)

            cx = pltpu.make_async_copy(x_hbm, xv, lsem.at[0])
            cg = pltpu.make_async_copy(g_hbm, gv, lsem.at[1])
            ci = pltpu.make_async_copy(ids_hbm, idv, lsem.at[2])
            cx.start()
            cg.start()
            ci.start()

            def w_copy(kt):
                return pltpu.make_async_copy(
                    w_hbm.at[pl.ds(pl.multiple_of(y * half, 16), half), pl.ds(pl.multiple_of(kt * TILE, TILE), TILE)],
                    wv.at[kt], wsem.at[kt])

            def tile_of(stream_t, i):
                return stream_t * ptiles + i

            order = []
            for k in range(ptiles + 2):
                for s, i in ((t, k), (far_t, k - 2), (sib_t, k), (nbr_t, k - 1)):
                    if 0 <= i < ptiles:
                        order.append(tile_of(s, i))
            for kt in order:
                w_copy(kt).start()

            barrier = pltpu.get_barrier_semaphore()
            peers = []
            for dy in range(2):
                for k in range(tp):
                    if dy or k:
                        peers.append((mate[0] if dy else d, lax.rem(t + k, tp), dy, k))
            for pd, pt, _, _ in peers:
                pl.semaphore_signal(barrier, inc=1, device_id=(pd, pt), device_id_type=MESH)

            def y_copy(i):
                return pltpu.make_async_remote_copy(
                    src_ref=nf.at[i], dst_ref=pf.at[t * parts + i], send_sem=ysend.at[i], recv_sem=yrecv.at[i],
                    device_id=mate, device_id_type=MESH)

            def x_copy(i, owner):
                kb = owner * parts + i
                return pltpu.make_async_remote_copy(
                    src_ref=pf.at[kb], dst_ref=pf.at[kb], send_sem=xsend.at[i], recv_sem=xrecv.at[i],
                    device_id=nbr, device_id_type=MESH)

            def a_copy(i, owner):
                kb = owner * parts + i
                return pltpu.make_async_remote_copy(
                    src_ref=pf.at[kb], dst_ref=pf.at[kb], send_sem=asend.at[i], recv_sem=arecv.at[i],
                    device_id=sib, device_id_type=MESH)

            def b_copy(i, owner):
                kb = owner * parts + i
                return pltpu.make_async_remote_copy(
                    src_ref=pf.at[kb], dst_ref=pf.at[kb], send_sem=bsend.at[i], recv_sem=brecv.at[i],
                    device_id=sib, device_id_type=MESH)

            id_copy = pltpu.make_async_remote_copy(
                src_ref=idv, dst_ref=idp, send_sem=isend, recv_sem=irecv, device_id=mate, device_id_type=MESH)

            nb[rows:LANES, :] = jnp.zeros((LANES - rows, dim), jnp.bfloat16)
            nb[LANES + rows:, :] = jnp.zeros((LANES - rows, dim), jnp.bfloat16)
            cg.wait()
            gf[...] = gv[...].astype(f32)
            cx.wait()
            sq = jnp.zeros((rows, LANES), f32)
            for k in range(kblocks):
                x = xv[:, k * LANES:(k + 1) * LANES].astype(f32)
                sq = sq + x * x
            inv = lax.rsqrt(jnp.sum(sq, axis=1, keepdims=True) / dim + NORM_EPS)

            def normed(kb):
                x = xv[:, pl.ds(pl.multiple_of(kb * LANES, LANES), LANES)].astype(f32)
                return (x * inv * gf[pl.ds(kb, 1), :]).astype(jnp.bfloat16)

            for i in range(parts):
                nf[i] = normed(t * parts + i).astype(f32)
            ci.wait()
            pl.semaphore_wait(barrier, len(peers))
            for i in range(parts):
                y_copy(i).start()
            id_copy.start()
            for k in range(kblocks):
                nb[:rows, k * LANES:(k + 1) * LANES] = normed(k)
            acc[...] = jnp.zeros_like(acc)

            def forward_y(i):
                y_copy(i).wait_recv()
                x_copy(i, t).start()
                a_copy(i, t).start()

            def forward_x(i):
                x_copy(i, nbr_t).wait_recv()
                b_copy(i, nbr_t).start()

            def load_tile(kt):
                w_copy(kt).wait()
                for h in range(2):
                    nb[LANES:LANES + rows, pl.ds(pl.multiple_of(kt * TILE + h * LANES, LANES), LANES)] = (
                        pf[2 * kt + h].astype(jnp.bfloat16))

            def tile_dot(kt, r):
                return lax.dot_general(wv[kt, r, :], nb[:, pl.ds(pl.multiple_of(kt * TILE, TILE), TILE)], NT,
                                       preferred_element_type=f32)

            forward_y(0)

            def step(p, _):
                k = p // 2
                first = lax.rem(p, 2) == 0

                @pl.when(p + 1 < parts)
                def _():
                    forward_y(p + 1)

                @pl.when((p >= 2) & (p - 2 < parts))
                def _():
                    forward_x(p - 2)

                late = jnp.where(first, k - 2, k - 1)
                early_on = k < ptiles
                late_on = late >= 0
                early_t = tile_of(jnp.where(first, t, sib_t), k)
                late_t = tile_of(jnp.where(first, far_t, nbr_t), late)

                @pl.when((p % 2 == 1) & early_on)
                def _():
                    a_copy(2 * k, sib_t).wait_recv()
                    a_copy(2 * k + 1, sib_t).wait_recv()

                @pl.when((p % 2 == 0) & late_on)
                def _():
                    b_copy(2 * late, far_t).wait_recv()
                    b_copy(2 * late + 1, far_t).wait_recv()

                @pl.when(early_on & late_on)
                def _():
                    load_tile(early_t)
                    load_tile(late_t)
                    for n in range(nblocks):
                        r = slice(n * BLOCK, (n + 1) * BLOCK)
                        acc[r, :] = acc[r, :] + (tile_dot(early_t, r) + tile_dot(late_t, r))

                @pl.when(jnp.logical_not(early_on & late_on))
                def _():
                    one = jnp.where(early_on, early_t, late_t)
                    load_tile(one)
                    for n in range(nblocks):
                        r = slice(n * BLOCK, (n + 1) * BLOCK)
                        acc[r, :] = acc[r, :] + tile_dot(one, r)

                return 0

            lax.fori_loop(0, 2 * ptiles + 2, step, 0)

            pad = jnp.full((1, LANES - drafts * batch), -1, jnp.int32)
            id_copy.wait_recv()
            ids = jnp.concatenate([idv[k:k + 1, :] for k in range(drafts)] + [pad]
                                  + [idp[k:k + 1, :] for k in range(drafts)] + [pad], axis=1)
            ids = ids - (t * cols + y * half)
            row_iota = lax.broadcasted_iota(jnp.int32, (BLOCK, TILE), 0)
            last_t = tile_of(far_t, ptiles - 1)
            b_copy(parts - 2, far_t).wait_recv()
            b_copy(parts - 1, far_t).wait_recv()
            load_tile(last_t)
            carry = None
            for n in range(nblocks):
                r = slice(n * BLOCK, (n + 1) * BLOCK)
                z = acc[r, :] + tile_dot(last_t, r)
                carry = update_stats(z, row_iota, ids - n * BLOCK, carry)
            packed = pack_stats(carry)
            slot = y * tp + t
            for k in range(4):
                st[0, k:k + 1, :] = packed[k][:, :LANES]
                st[1, k:k + 1, :] = packed[k][:, LANES:]
                rs[slot, k:k + 1, :] = packed[k][:, :LANES]

            def s_copy(pd, pt, dy, k, into):
                return pltpu.make_async_remote_copy(
                    src_ref=st.at[dy], dst_ref=rs.at[into], send_sem=ssem.at[dy * tp + k], recv_sem=rsem.at[into],
                    device_id=(pd, pt), device_id_type=MESH)

            for pd, pt, dy, k in peers:
                s_copy(pd, pt, dy, k, slot).start()
            for i in range(parts):
                y_copy(i).wait_send()
                x_copy(i, t).wait_send()
                a_copy(i, t).wait_send()
                b_copy(i, nbr_t).wait_send()
            id_copy.wait_send()
            for pd, pt, dy, k in peers:
                s_copy(pd, pt, dy, k, (1 - y if dy else y) * tp + pt).wait_recv()
            ms = [rs[k, 0:1, :] for k in range(2 * tp)]
            top = ms[0]
            for k in range(1, 2 * tp):
                top = jnp.maximum(top, ms[k])
            s = jnp.zeros((1, LANES), f32)
            w = s
            p = s
            for k in range(2 * tp):
                dm = ms[k] - top
                f = jnp.exp(dm)
                s = s + f * rs[k, 1:2, :]
                w = w + f * (rs[k, 2:3, :] + dm * rs[k, 1:2, :])
                p = p + rs[k, 3:4, :]
            log_sum = jnp.log(s)
            log_norm = top + log_sum
            ent = log_sum - w / s
            logp = p - log_norm
            for k in range(pos):
                o_logn[k:k + 1, :] = log_norm[:, k * batch:(k + 1) * batch]
                o_ent[k:k + 1, :] = ent[:, k * batch:(k + 1) * batch]
            for k in range(drafts):
                o_logp[k:k + 1, :] = logp[:, k * batch:(k + 1) * batch]
            for pd, pt, dy, k in peers:
                s_copy(pd, pt, dy, k, slot).wait_send()

        hbm = pl.BlockSpec(memory_space=pl.ANY)
        vmem = pl.BlockSpec(memory_space=pltpu.VMEM)
        dma = pltpu.SemaphoreType.DMA
        bf16 = jnp.bfloat16
        logp, logn, ent = pl.pallas_call(
            kernel,
            out_shape=[jax.ShapeDtypeStruct((drafts, batch), f32), jax.ShapeDtypeStruct((pos, batch), f32),
                       jax.ShapeDtypeStruct((pos, batch), f32)],
            in_specs=[hbm] * 4,
            out_specs=[vmem] * 3,
            scratch_shapes=[
                pltpu.VMEM((tiles, half, TILE), bf16),
                pltpu.VMEM((rows, dim), bf16),
                pltpu.VMEM((2 * LANES, dim), bf16),
                pltpu.VMEM((parts, rows, LANES), f32),
                pltpu.VMEM((kblocks, rows, LANES), f32),
                pltpu.VMEM((half, 2 * LANES), f32),
                pltpu.VMEM((kblocks, LANES), bf16),
                pltpu.VMEM((kblocks, LANES), f32),
                pltpu.VMEM((drafts, batch), jnp.int32),
                pltpu.VMEM((drafts, batch), jnp.int32),
                pltpu.VMEM((2, 8, LANES), f32),
                pltpu.VMEM((2 * tp, 8, LANES), f32),
                dma((tiles,)),
                dma((3,)),
                dma((parts,)), dma((parts,)),
                dma((parts,)), dma((parts,)),
                dma((parts,)), dma((parts,)),
                dma((parts,)), dma((parts,)),
                dma, dma,
                dma((2 * tp,)), dma((2 * tp,)),
            ],
            compiler_params=pltpu.CompilerParams(
                collective_id=0, has_side_effects=True, vmem_limit_bytes=62 * 1024 * 1024),
        )(hidden.transpose(1, 0, 2).reshape(rows, dim), draft_ids.T, norm_gain.reshape(kblocks, LANES), head_w.T)
        return logp.T, logn.T, ent.T

    specs_in = (P('dp', None, None), P('dp', None), P(None), P(None, 'tp'))
    specs_out = (P('dp', None), P('dp', None), P('dp', None))
    return jax.shard_map(per_device, mesh=mesh, in_specs=specs_in, out_specs=specs_out, check_vma=False)
```

time: 45.7 us -> 44.2 us (0.967)
  Pallas kernels: 41.1 us -> 39.6 us
    pallas_call x1, Pallas kernels: 41.1 us -> 39.6 us  [per_device(): pl.pallas_call(kernel, out_shape=[jax.ShapeDtypeStruct((drafts, batch), f...]
where the time goes in v2:
time: 44.2 us; the launch traced here: 44 us
  Pallas kernels  39.6 us (90%)
  local copies, waits for them, and re-layouts  3.77 us (9%)
  between operations  0.64 us (1%)
    pallas_call x1, Pallas kernels, per_device(): pl.pallas_call(kernel, out_shape=[jax.ShapeDtypeStruct((drafts, batch), f...  39.6 us
    unnamed x3, local copies, waits for them, and re-layouts  3.77 us

profile of v2, /device:TPU:0, one launch (start us, length us, event | category | flops | bytes accessed | tf_op | source)
XLA Modules:
  0.0 44.0 jit_solution(5663478717502720053)
XLA Ops:
  0.6 39.6 %shard_map.67 = (f32[4,16]{1,0:T(4,128)}, f32[5,16]{1,0:T(8,128)}, f32[5,16]{1,0:T(8,128)}) custom-call(bf16[80,5120]{1,0:T(8,128)(2,1)} %bitcast.9, s32[4,16]{1,0:T(4,128)} %bitcast.13, bf16[40,128]{1,0:T(8,128)(2,1)} %bitcast.10, bf16[8000,5120]{1,0:T(8,128)(2,1)} %bitcast.4.w_hbm), custom_call_target="tpu_custom_call" | custom-call | tf_op jit(solution)/shard_map/pallas_call | solution.py:305
  40.2 1.2 %copy.10 = f32[16,4]{0,1:T(4,128)} copy(f32[16,4]{0,1:T(4,128)} %bitcast.14) | data formatting | bytes 512
  41.4 1.3 %copy.11 = f32[16,5]{0,1:T(8,128)} copy(f32[16,5]{0,1:T(8,128)} %bitcast.12) | data formatting | bytes 640
  42.7 1.3 %copy.12 = f32[16,5]{0,1:T(8,128)} copy(f32[16,5]{0,1:T(8,128)} %bitcast.11) | data formatting | bytes 640

commit v3 on v2

--- a/solution.py
+++ b/solution.py
@@ -10,6 +10,10 @@
 LANES = 128
 TILE = 256
 BLOCK = 800
+OWN = 1600
+CHUNK = 400
+AHEAD = 2
+DEPTH = 4
 NT = (((1,), (1,)), ((), ()))
 
 
@@ -21,7 +25,7 @@
     return jnp.max(block.reshape(-1, 8, block.shape[-1]), axis=0)
 
 
-def update_stats(z, row_ids, ids, carry):
+def update_stats(z, row_ids, ids, carry, first=None):
     bm = rows_max(z)
     z3 = z.reshape(-1, 8, z.shape[-1])
     picked = rows_sum(jnp.where(row_ids == ids, z, 0.0))
@@ -30,6 +34,8 @@
         e = jnp.exp(sh)
         return bm, jnp.sum(e, axis=0), jnp.sum(e * sh, axis=0), picked
     m, s, w, p = carry
+    if first is not None:
+        m = jnp.where(first, bm, m)
     mn = jnp.maximum(m, bm)
     dm = m - mn
     a = jnp.exp(dm)
@@ -38,6 +44,18 @@
     w = a * (w + dm * s) + jnp.sum(e * sh, axis=0)
     s = a * s + jnp.sum(e, axis=0)
     return mn, s, w, p + picked
+
+
+def merge_stats(a, b):
+    top = jnp.maximum(a[0], b[0])
+    da, db = a[0] - top, b[0] - top
+    fa, fb = jnp.exp(da), jnp.exp(db)
+    return (
+        top,
+        fa * a[1] + fb * b[1],
+        fa * (a[2] + da * a[1]) + fb * (b[2] + db * b[1]),
+        a[3] + b[3],
+    )
 
 
 def pack_stats(carry):
@@ -60,7 +78,8 @@
         batch, pos, dim = hidden.shape
         drafts = draft_ids.shape[1]
         cols = head_w.shape[1]
-        half = cols // 2
+        half = (cols - OWN) // 2
+        chunks = OWN // CHUNK
         rows = batch * pos
         kblocks = dim // LANES
         tiles = dim // TILE
@@ -69,9 +88,9 @@
         nblocks = half // BLOCK
         f32 = jnp.float32
 
-        def kernel(x_hbm, ids_hbm, g_hbm, w_hbm, o_logp, o_logn, o_ent,
-                   wv, xv, nb, nf, pf, acc, gv, gf, idv, idp, st, rs,
-                   wsem, lsem, ysend, yrecv, xsend, xrecv, asend, arecv, bsend, brecv, isend, irecv, ssem, rsem):
+        def kernel(x_hbm, ids_hbm, g_hbm, w_hbm, out,
+                   ev, wv, xv, nb, nf, pf, acc, gv, gf, idv, idp, st, rs,
+                   esem, wsem, lsem, ysend, yrecv, xsend, xrecv, asend, arecv, bsend, brecv, isend, irecv, ssem, rsem):
             t = lax.axis_index('tp')
             d = lax.axis_index('dp')
             y = lax.rem(d, 2)
@@ -92,20 +111,36 @@
 
             def w_copy(kt):
                 return pltpu.make_async_copy(
-                    w_hbm.at[pl.ds(pl.multiple_of(y * half, 16), half), pl.ds(pl.multiple_of(kt * TILE, TILE), TILE)],
+                    w_hbm.at[pl.ds(pl.multiple_of(OWN + y * half, 16), half), pl.ds(pl.multiple_of(kt * TILE, TILE), TILE)],
                     wv.at[kt], wsem.at[kt])
 
             def tile_of(stream_t, i):
                 return stream_t * ptiles + i
 
-            order = []
-            for k in range(ptiles + 2):
-                for s, i in ((t, k), (far_t, k - 2), (sib_t, k), (nbr_t, k - 1)):
-                    if 0 <= i < ptiles:
-                        order.append(tile_of(s, i))
-            for kt in order:
-                w_copy(kt).start()
-
+            def plan(p):
+                k = p // 2
+                first = lax.rem(p, 2) == 0
+                late = jnp.where(first, k - 2, k - 1)
+                early_t = tile_of(jnp.where(first, t, sib_t), k)
+                late_t = tile_of(jnp.where(first, far_t, nbr_t), late)
+                return k, late, early_t, late_t, k < ptiles, (late >= 0) & (late < ptiles)
+
+            def w_start(p):
+                _, _, early_t, late_t, early_on, late_on = plan(p)
+
+                @pl.when(early_on)
+                def _():
+                    w_copy(early_t).start()
+
+                @pl.when(late_on)
+                def _():
+                    w_copy(late_t).start()
+
+            def e_copy(e):
+                return pltpu.make_async_copy(
+                    w_hbm.at[pl.ds(pl.multiple_of(e * CHUNK, 16), CHUNK), :], ev.at[e], esem.at[e])
+
+            e_copy(0).start()
             barrier = pltpu.get_barrier_semaphore()
             peers = []
             for dy in range(2):
@@ -143,9 +178,13 @@
 
             nb[rows:LANES, :] = jnp.zeros((LANES - rows, dim), jnp.bfloat16)
             nb[LANES + rows:, :] = jnp.zeros((LANES - rows, dim), jnp.bfloat16)
-            cg.wait()
+            with jax.named_scope('waitg'):
+                ci.wait()
+                cg.wait()
             gf[...] = gv[...].astype(f32)
-            cx.wait()
+            with jax.named_scope('waitx'):
+                cx.wait()
+            e_copy(1).start()
             sq = jnp.zeros((rows, LANES), f32)
             for k in range(kblocks):
                 x = xv[:, k * LANES:(k + 1) * LANES].astype(f32)
@@ -158,8 +197,8 @@
 
             for i in range(parts):
                 nf[i] = normed(t * parts + i).astype(f32)
-            ci.wait()
-            pl.semaphore_wait(barrier, len(peers))
+            with jax.named_scope('barr'):
+                pl.semaphore_wait(barrier, len(peers))
             for i in range(parts):
                 y_copy(i).start()
             id_copy.start()
@@ -177,7 +216,8 @@
                 b_copy(i, nbr_t).start()
 
             def load_tile(kt):
-                w_copy(kt).wait()
+                with jax.named_scope('ww'):
+                    w_copy(kt).wait()
                 for h in range(2):
                     nb[LANES:LANES + rows, pl.ds(pl.multiple_of(kt * TILE + h * LANES, LANES), LANES)] = (
                         pf[2 * kt + h].astype(jnp.bfloat16))
@@ -186,77 +226,119 @@
                 return lax.dot_general(wv[kt, r, :], nb[:, pl.ds(pl.multiple_of(kt * TILE, TILE), TILE)], NT,
                                        preferred_element_type=f32)
 
-            forward_y(0)
+            own_ids = jnp.concatenate([idv[k:k + 1, :] for k in range(drafts)]
+                                      + [jnp.full((1, LANES - drafts * batch), -1, jnp.int32)], axis=1) - t * cols
+            own_iota = lax.broadcasted_iota(jnp.int32, (CHUNK, LANES), 0)
+
+            def own_step(e, carry):
+                with jax.named_scope('waite'):
+                    e_copy(e).wait()
+
+                @pl.when(e + 2 < chunks)
+                def _():
+                    e_copy(e + 2).start()
+
+                @pl.when(e == chunks - 2)
+                def _():
+                    w_start(0)
+                    w_start(1)
+
+                @pl.when(e == chunks - 1)
+                def _():
+                    w_start(2)
+                    w_start(3)
+
+                with jax.named_scope('own'):
+                    z = lax.dot_general(ev[e], nb[:LANES, :], NT, preferred_element_type=f32)
+                    carry = update_stats(z, own_iota, own_ids - e * CHUNK, carry, e == 0)
+
+                @pl.when(e >= chunks - AHEAD)
+                def _():
+                    with jax.named_scope('fyo'):
+                        forward_y(e - (chunks - AHEAD))
+
+                return carry
+
+            zero = jnp.zeros((8, LANES), f32)
+            own_carry = lax.fori_loop(0, chunks, own_step, (zero, zero, zero, zero))
+
+            last_p = 2 * ptiles + 2
 
             def step(p, _):
-                k = p // 2
-                first = lax.rem(p, 2) == 0
-
-                @pl.when(p + 1 < parts)
-                def _():
-                    forward_y(p + 1)
+                k, late, early_t, late_t, early_on, late_on = plan(p)
+
+                @pl.when(p + DEPTH <= last_p)
+                def _():
+                    w_start(p + DEPTH)
+
+                @pl.when(p + AHEAD < parts)
+                def _():
+                    with jax.named_scope('fy'):
+                        forward_y(p + AHEAD)
 
                 @pl.when((p >= 2) & (p - 2 < parts))
                 def _():
-                    forward_x(p - 2)
-
-                late = jnp.where(first, k - 2, k - 1)
-                early_on = k < ptiles
-                late_on = late >= 0
-                early_t = tile_of(jnp.where(first, t, sib_t), k)
-                late_t = tile_of(jnp.where(first, far_t, nbr_t), late)
+                    with jax.named_scope('fx'):
+                        forward_x(p - 2)
 
                 @pl.when((p % 2 == 1) & early_on)
                 def _():
-                    a_copy(2 * k, sib_t).wait_recv()
-                    a_copy(2 * k + 1, sib_t).wait_recv()
+                    with jax.named_scope('wa'):
+                        a_copy(2 * k, sib_t).wait_recv()
+                        a_copy(2 * k + 1, sib_t).wait_recv()
 
                 @pl.when((p % 2 == 0) & late_on)
                 def _():
-                    b_copy(2 * late, far_t).wait_recv()
-                    b_copy(2 * late + 1, far_t).wait_recv()
+                    with jax.named_scope('wb'):
+                        b_copy(2 * late, far_t).wait_recv()
+                        b_copy(2 * late + 1, far_t).wait_recv()
 
                 @pl.when(early_on & late_on)
                 def _():
                     load_tile(early_t)
                     load_tile(late_t)
-                    for n in range(nblocks):
-                        r = slice(n * BLOCK, (n + 1) * BLOCK)
-                        acc[r, :] = acc[r, :] + (tile_dot(early_t, r) + tile_dot(late_t, r))
+                    with jax.named_scope('dual'):
+                        for n in range(nblocks):
+                            r = slice(n * BLOCK, (n + 1) * BLOCK)
+                            acc[r, :] = acc[r, :] + (tile_dot(early_t, r) + tile_dot(late_t, r))
 
                 @pl.when(jnp.logical_not(early_on & late_on))
                 def _():
                     one = jnp.where(early_on, early_t, late_t)
                     load_tile(one)
-                    for n in range(nblocks):
-                        r = slice(n * BLOCK, (n + 1) * BLOCK)
-                        acc[r, :] = acc[r, :] + tile_dot(one, r)
+                    with jax.named_scope('single'):
+                        for n in range(nblocks):
+                            r = slice(n * BLOCK, (n + 1) * BLOCK)
+                            acc[r, :] = acc[r, :] + tile_dot(one, r)
 
                 return 0
 
-            lax.fori_loop(0, 2 * ptiles + 2, step, 0)
+            lax.fori_loop(0, last_p, step, 0)
 
             pad = jnp.full((1, LANES - drafts * batch), -1, jnp.int32)
             id_copy.wait_recv()
             ids = jnp.concatenate([idv[k:k + 1, :] for k in range(drafts)] + [pad]
                                   + [idp[k:k + 1, :] for k in range(drafts)] + [pad], axis=1)
-            ids = ids - (t * cols + y * half)
+            ids = ids - (t * cols + OWN + y * half)
             row_iota = lax.broadcasted_iota(jnp.int32, (BLOCK, TILE), 0)
             last_t = tile_of(far_t, ptiles - 1)
-            b_copy(parts - 2, far_t).wait_recv()
-            b_copy(parts - 1, far_t).wait_recv()
+            with jax.named_scope('wlast'):
+                b_copy(parts - 2, far_t).wait_recv()
+                b_copy(parts - 1, far_t).wait_recv()
             load_tile(last_t)
             carry = None
-            for n in range(nblocks):
-                r = slice(n * BLOCK, (n + 1) * BLOCK)
-                z = acc[r, :] + tile_dot(last_t, r)
-                carry = update_stats(z, row_iota, ids - n * BLOCK, carry)
-            packed = pack_stats(carry)
+            with jax.named_scope('final'):
+                for n in range(nblocks):
+                    r = slice(n * BLOCK, (n + 1) * BLOCK)
+                    z = acc[r, :] + tile_dot(last_t, r)
+                    carry = update_stats(z, row_iota, ids - n * BLOCK, carry)
+            mine = pack_stats(merge_stats(own_carry, [c[:, :LANES] for c in carry]))
+            theirs = pack_stats([c[:, LANES:] for c in carry])
             slot = y * tp + t
             for k in range(4):
-                st[0, k:k + 1, :] = packed[k][:, :LANES]
-                st[1, k:k + 1, :] = packed[k][:, LANES:]
-                rs[slot, k:k + 1, :] = packed[k][:, :LANES]
+                st[0, k:k + 1, :] = mine[k]
+                st[1, k:k + 1, :] = theirs[k]
+                rs[slot, k:k + 1, :] = mine[k]
 
             def s_copy(pd, pt, dy, k, into):
                 return pltpu.make_async_remote_copy(
@@ -271,8 +353,9 @@
                 a_copy(i, t).wait_send()
                 b_copy(i, nbr_t).wait_send()
             id_copy.wait_send()
-            for pd, pt, dy, k in peers:
-                s_copy(pd, pt, dy, k, (1 - y if dy else y) * tp + pt).wait_recv()
+            with jax.named_scope('wstat'):
+                for pd, pt, dy, k in peers:
+                    s_copy(pd, pt, dy, k, (1 - y if dy else y) * tp + pt).wait_recv()
             ms = [rs[k, 0:1, :] for k in range(2 * tp)]
             top = ms[0]
             for k in range(1, 2 * tp):
@@ -291,10 +374,9 @@
             ent = log_sum - w / s
             logp = p - log_norm
             for k in range(pos):
-                o_logn[k:k + 1, :] = log_norm[:, k * batch:(k + 1) * batch]
-                o_ent[k:k + 1, :] = ent[:, k * batch:(k + 1) * batch]
-            for k in range(drafts):
-                o_logp[k:k + 1, :] = logp[:, k * batch:(k + 1) * batch]
+                out[k:k + 1, :] = log_norm[:, k * batch:(k + 1) * batch]
+                out[pos + k:pos + k + 1, :] = ent[:, k * batch:(k + 1) * batch]
+                out[2 * pos + k:2 * pos + k + 1, :] = logp[:, k * batch:(k + 1) * batch]
             for pd, pt, dy, k in peers:
                 s_copy(pd, pt, dy, k, slot).wait_send()
 
@@ -302,13 +384,13 @@
         vmem = pl.BlockSpec(memory_space=pltpu.VMEM)
         dma = pltpu.SemaphoreType.DMA
         bf16 = jnp.bfloat16
-        logp, logn, ent = pl.pallas_call(
+        packed = pl.pallas_call(
             kernel,
-            out_shape=[jax.ShapeDtypeStruct((drafts, batch), f32), jax.ShapeDtypeStruct((pos, batch), f32),
-                       jax.ShapeDtypeStruct((pos, batch), f32)],
+            out_shape=jax.ShapeDtypeStruct((3 * pos, batch), f32),
             in_specs=[hbm] * 4,
-            out_specs=[vmem] * 3,
+            out_specs=vmem,
             scratch_shapes=[
+                pltpu.VMEM((chunks, CHUNK, dim), bf16),
                 pltpu.VMEM((tiles, half, TILE), bf16),
                 pltpu.VMEM((rows, dim), bf16),
                 pltpu.VMEM((2 * LANES, dim), bf16),
@@ -321,6 +403,7 @@
                 pltpu.VMEM((drafts, batch), jnp.int32),
                 pltpu.VMEM((2, 8, LANES), f32),
                 pltpu.VMEM((2 * tp, 8, LANES), f32),
+                dma((chunks,)),
                 dma((tiles,)),
                 dma((3,)),
                 dma((parts,)), dma((parts,)),
@@ -331,8 +414,21 @@
                 dma((2 * tp,)), dma((2 * tp,)),
             ],
             compiler_params=pltpu.CompilerParams(
-                collective_id=0, has_side_effects=True, vmem_limit_bytes=62 * 1024 * 1024),
+                collective_id=0, has_side_effects=True, vmem_limit_bytes=60 * 1024 * 1024),
         )(hidden.transpose(1, 0, 2).reshape(rows, dim), draft_ids.T, norm_gain.reshape(kblocks, LANES), head_w.T)
+
+        def split(src, o_logp, o_logn, o_ent):
+            o_logn[...] = src[:pos, :]
+            o_ent[...] = src[pos:2 * pos, :]
+            o_logp[...] = src[2 * pos:2 * pos + drafts, :]
+
+        logp, logn, ent = pl.pallas_call(
+            split,
+            out_shape=[jax.ShapeDtypeStruct((drafts, batch), f32), jax.ShapeDtypeStruct((pos, batch), f32),
+                       jax.ShapeDtypeStruct((pos, batch), f32)],
+            in_specs=[vmem],
+            out_specs=[vmem] * 3,
+        )(packed)
         return logp.T, logn.T, ent.T
 
     specs_in = (P('dp', None, None), P('dp', None), P(None), P(None, 'tp'))

time: 44.2 us -> 31.6 us (0.71)
  Pallas kernels: 39.6 us -> 30.8 us
  local copies, waits for them, and re-layouts: 3.77 us -> 0 us
    pallas_call x1 -> x2, Pallas kernels: 39.6 us -> 30.8 us  [the longest x1 29.5 us: per_device(): pl.pallas_call(kernel, out_shape=jax.ShapeDtypeStruct((3 * pos, batch), f...]
    unnamed x3 -> x0, local copies, waits for them, and re-layouts: 3.77 us -> none
where the time goes in v3:
time: 31.6 us; the launch traced here: 31.4 us
  Pallas kernels  30.8 us (97%)
  between operations  0.64 us (2%)
    pallas_call x1, Pallas kernels, per_device(): pl.pallas_call(kernel, out_shape=jax.ShapeDtypeStruct((3 * pos, batch), f...  29.5 us
    pallas_call x1, Pallas kernels, per_device(): pl.pallas_call(split, out_shape=[jax.ShapeDtypeStruct((drafts, batch), f3...  1.3 us

profile of v3, /device:TPU:0, one launch (start us, length us, event | category | flops | bytes accessed | tf_op | source)
XLA Modules:
  0.0 31.4 jit_solution(5953298349335925244)
XLA Ops:
  0.6 29.5 %shard_map.67.src = f32[15,16]{1,0:T(8,128)} custom-call(bf16[80,5120]{1,0:T(8,128)(2,1)} %bitcast.9, s32[4,16]{1,0:T(4,128)} %bitcast.11, bf16[40,128]{1,0:T(8,128)(2,1)} %bitcast.10, bf16[8000,5120]{1,0:T(8,128)(2,1)} %bitcast.4.w_hbm), custom_call_target="tpu_custom_call" | custom-call | tf_op jit(solution)/shard_map/pallas_call | solution.py:387
  30.1 1.3 %shard_map.68 = (f32[4,16]{1,0:T(4,128)}, f32[5,16]{1,0:T(8,128)}, f32[5,16]{1,0:T(8,128)}) custom-call(f32[15,16]{1,0:T(8,128)} %shard_map.67.src), custom_call_target="tpu_custom_call" | custom-call | tf_op jit(solution)/shard_map/pallas_call | solution.py:425

commit v4 on v3

--- a/solution.py
+++ b/solution.py
@@ -12,8 +12,18 @@
 BLOCK = 800
 OWN = 1600
 CHUNK = 400
-AHEAD = 2
-DEPTH = 4
+DEPTH = 6
+OWN_FORWARDS = ((), (0,), (1, 2), (3,))
+STEPS = (
+    ((), (), ('y0', 'y1')),
+    ((4,), (0,), ('a0', 'a1')),
+    ((5, 6), (1, 2), ('x0', 'y2')),
+    ((7,), (3,), ('b0', 'a2', 'x1')),
+    ((8, 9), (4,), ('y3', 'y4', 'a3', 'b1')),
+    ((), (5, 6, 7), ('x2', 'x3', 'a4')),
+    ((), (8, 9), ('b2', 'b3', 'x4')),
+    ((), (), ('b4',)),
+)
 NT = (((1,), (1,)), ((), ()))
 
 
@@ -117,24 +127,12 @@
             def tile_of(stream_t, i):
                 return stream_t * ptiles + i
 
-            def plan(p):
-                k = p // 2
-                first = lax.rem(p, 2) == 0
-                late = jnp.where(first, k - 2, k - 1)
-                early_t = tile_of(jnp.where(first, t, sib_t), k)
-                late_t = tile_of(jnp.where(first, far_t, nbr_t), late)
-                return k, late, early_t, late_t, k < ptiles, (late >= 0) & (late < ptiles)
-
-            def w_start(p):
-                _, _, early_t, late_t, early_on, late_on = plan(p)
-
-                @pl.when(early_on)
-                def _():
-                    w_copy(early_t).start()
-
-                @pl.when(late_on)
-                def _():
-                    w_copy(late_t).start()
+            stream_t = {'y': t, 'a': sib_t, 'x': nbr_t, 'b': far_t}
+
+            def kt_of(name):
+                return tile_of(stream_t[name[0]], int(name[1:]))
+
+            order = [name for _, _, names in STEPS for name in names]
 
             def e_copy(e):
                 return pltpu.make_async_copy(
@@ -152,25 +150,25 @@
 
             def y_copy(i):
                 return pltpu.make_async_remote_copy(
-                    src_ref=nf.at[i], dst_ref=pf.at[t * parts + i], send_sem=ysend.at[i], recv_sem=yrecv.at[i],
+                    src_ref=nf.at[i], dst_ref=pf.at[t * parts + i], send_sem=ysend, recv_sem=yrecv.at[i],
                     device_id=mate, device_id_type=MESH)
 
             def x_copy(i, owner):
                 kb = owner * parts + i
                 return pltpu.make_async_remote_copy(
-                    src_ref=pf.at[kb], dst_ref=pf.at[kb], send_sem=xsend.at[i], recv_sem=xrecv.at[i],
+                    src_ref=pf.at[kb], dst_ref=pf.at[kb], send_sem=xsend, recv_sem=xrecv.at[i],
                     device_id=nbr, device_id_type=MESH)
 
             def a_copy(i, owner):
                 kb = owner * parts + i
                 return pltpu.make_async_remote_copy(
-                    src_ref=pf.at[kb], dst_ref=pf.at[kb], send_sem=asend.at[i], recv_sem=arecv.at[i],
+                    src_ref=pf.at[kb], dst_ref=pf.at[kb], send_sem=asend, recv_sem=arecv.at[i],
                     device_id=sib, device_id_type=MESH)
 
             def b_copy(i, owner):
                 kb = owner * parts + i
                 return pltpu.make_async_remote_copy(
-                    src_ref=pf.at[kb], dst_ref=pf.at[kb], send_sem=bsend.at[i], recv_sem=brecv.at[i],
+                    src_ref=pf.at[kb], dst_ref=pf.at[kb], send_sem=bsend, recv_sem=brecv.at[i],
                     device_id=sib, device_id_type=MESH)
 
             id_copy = pltpu.make_async_remote_copy(
@@ -204,7 +202,6 @@
             id_copy.start()
             for k in range(kblocks):
                 nb[:rows, k * LANES:(k + 1) * LANES] = normed(k)
-            acc[...] = jnp.zeros_like(acc)
 
             def forward_y(i):
                 y_copy(i).wait_recv()
@@ -215,16 +212,32 @@
                 x_copy(i, nbr_t).wait_recv()
                 b_copy(i, nbr_t).start()
 
-            def load_tile(kt):
+            def load_tile(name):
+                kt = kt_of(name)
+                nxt = order.index(name) + DEPTH
+                if nxt < len(order):
+                    w_copy(kt_of(order[nxt])).start()
+                i = int(name[1:])
+                with jax.named_scope('wait_' + name):
+                    for h in range(2):
+                        if name[0] == 'a':
+                            a_copy(2 * i + h, sib_t).wait_recv()
+                        if name[0] == 'b':
+                            b_copy(2 * i + h, far_t).wait_recv()
                 with jax.named_scope('ww'):
                     w_copy(kt).wait()
                 for h in range(2):
                     nb[LANES:LANES + rows, pl.ds(pl.multiple_of(kt * TILE + h * LANES, LANES), LANES)] = (
                         pf[2 * kt + h].astype(jnp.bfloat16))
 
-            def tile_dot(kt, r):
-                return lax.dot_general(wv[kt, r, :], nb[:, pl.ds(pl.multiple_of(kt * TILE, TILE), TILE)], NT,
-                                       preferred_element_type=f32)
+            def tiles_dot(names, r):
+                z = None
+                for name in names:
+                    kt = kt_of(name)
+                    one = lax.dot_general(wv[kt, r, :], nb[:, pl.ds(pl.multiple_of(kt * TILE, TILE), TILE)], NT,
+                                          preferred_element_type=f32)
+                    z = one if z is None else z + one
+                return z
 
             own_ids = jnp.concatenate([idv[k:k + 1, :] for k in range(drafts)]
                                       + [jnp.full((1, LANES - drafts * batch), -1, jnp.int32)], axis=1) - t * cols
@@ -240,80 +253,46 @@
 
                 @pl.when(e == chunks - 2)
                 def _():
-                    w_start(0)
-                    w_start(1)
+                    for name in order[:DEPTH // 2]:
+                        w_copy(kt_of(name)).start()
 
                 @pl.when(e == chunks - 1)
                 def _():
-                    w_start(2)
-                    w_start(3)
+                    for name in order[DEPTH // 2:DEPTH]:
+                        w_copy(kt_of(name)).start()
 
                 with jax.named_scope('own'):
                     z = lax.dot_general(ev[e], nb[:LANES, :], NT, preferred_element_type=f32)
                     carry = update_stats(z, own_iota, own_ids - e * CHUNK, carry, e == 0)
-
-                @pl.when(e >= chunks - AHEAD)
-                def _():
-                    with jax.named_scope('fyo'):
-                        forward_y(e - (chunks - AHEAD))
-
+                for chunk, blocks in enumerate(OWN_FORWARDS):
+                    if blocks:
+                        @pl.when(e == chunk)
+                        def _():
+                            with jax.named_scope('fy'):
+                                for i in blocks:
+                                    forward_y(i)
                 return carry
 
             zero = jnp.zeros((8, LANES), f32)
             own_carry = lax.fori_loop(0, chunks, own_step, (zero, zero, zero, zero))
 
-            last_p = 2 * ptiles + 2
-
-            def step(p, _):
-                k, late, early_t, late_t, early_on, late_on = plan(p)
-
-                @pl.when(p + DEPTH <= last_p)
+            for n_step, (ys, xs, names) in enumerate(STEPS[:-1]):
+                for i in ys:
+                    with jax.named_scope('fy'):
+                        forward_y(i)
+                for i in xs:
+                    with jax.named_scope('fx'):
+                        forward_x(i)
+                for name in names:
+                    load_tile(name)
+
+                @pl.when(t >= 0)
                 def _():
-                    w_start(p + DEPTH)
-
-                @pl.when(p + AHEAD < parts)
-                def _():
-                    with jax.named_scope('fy'):
-                        forward_y(p + AHEAD)
-
-                @pl.when((p >= 2) & (p - 2 < parts))
-                def _():
-                    with jax.named_scope('fx'):
-                        forward_x(p - 2)
-
-                @pl.when((p % 2 == 1) & early_on)
-                def _():
-                    with jax.named_scope('wa'):
-                        a_copy(2 * k, sib_t).wait_recv()
-                        a_copy(2 * k + 1, sib_t).wait_recv()
-
-                @pl.when((p % 2 == 0) & late_on)
-                def _():
-                    with jax.named_scope('wb'):
-                        b_copy(2 * late, far_t).wait_recv()
-                        b_copy(2 * late + 1, far_t).wait_recv()
-
-                @pl.when(early_on & late_on)
-                def _():
-                    load_tile(early_t)
-                    load_tile(late_t)
-                    with jax.named_scope('dual'):
+                    with jax.named_scope('step'):
                         for n in range(nblocks):
                             r = slice(n * BLOCK, (n + 1) * BLOCK)
-                            acc[r, :] = acc[r, :] + (tile_dot(early_t, r) + tile_dot(late_t, r))
-
-                @pl.when(jnp.logical_not(early_on & late_on))
-                def _():
-                    one = jnp.where(early_on, early_t, late_t)
-                    load_tile(one)
-                    with jax.named_scope('single'):
-                        for n in range(nblocks):
-                            r = slice(n * BLOCK, (n + 1) * BLOCK)
-                            acc[r, :] = acc[r, :] + tile_dot(one, r)
-
-                return 0
-
-            lax.fori_loop(0, last_p, step, 0)
+                            z = tiles_dot(names, r)
+                            acc[r, :] = z if n_step == 0 else acc[r, :] + z
 
             pad = jnp.full((1, LANES - drafts * batch), -1, jnp.int32)
             id_copy.wait_recv()
@@ -321,16 +300,12 @@
                                   + [idp[k:k + 1, :] for k in range(drafts)] + [pad], axis=1)
             ids = ids - (t * cols + OWN + y * half)
             row_iota = lax.broadcasted_iota(jnp.int32, (BLOCK, TILE), 0)
-            last_t = tile_of(far_t, ptiles - 1)
-            with jax.named_scope('wlast'):
-                b_copy(parts - 2, far_t).wait_recv()
-                b_copy(parts - 1, far_t).wait_recv()
-            load_tile(last_t)
+            load_tile(order[-1])
             carry = None
             with jax.named_scope('final'):
                 for n in range(nblocks):
                     r = slice(n * BLOCK, (n + 1) * BLOCK)
-                    z = acc[r, :] + tile_dot(last_t, r)
+                    z = acc[r, :] + tiles_dot(order[-1:], r)
                     carry = update_stats(z, row_iota, ids - n * BLOCK, carry)
             mine = pack_stats(merge_stats(own_carry, [c[:, :LANES] for c in carry]))
             theirs = pack_stats([c[:, LANES:] for c in carry])
@@ -342,43 +317,44 @@
 
             def s_copy(pd, pt, dy, k, into):
                 return pltpu.make_async_remote_copy(
-                    src_ref=st.at[dy], dst_ref=rs.at[into], send_sem=ssem.at[dy * tp + k], recv_sem=rsem.at[into],
+                    src_ref=st.at[dy], dst_ref=rs.at[into], send_sem=ssem, recv_sem=rsem.at[into],
                     device_id=(pd, pt), device_id_type=MESH)
 
             for pd, pt, dy, k in peers:
                 s_copy(pd, pt, dy, k, slot).start()
-            for i in range(parts):
-                y_copy(i).wait_send()
-                x_copy(i, t).wait_send()
-                a_copy(i, t).wait_send()
-                b_copy(i, nbr_t).wait_send()
+            for sem in (ysend, xsend, asend, bsend):
+                pltpu.make_async_remote_copy(
+                    src_ref=nf, dst_ref=nf, send_sem=sem, recv_sem=irecv, device_id=sib, device_id_type=MESH).wait_send()
             id_copy.wait_send()
             with jax.named_scope('wstat'):
                 for pd, pt, dy, k in peers:
                     s_copy(pd, pt, dy, k, (1 - y if dy else y) * tp + pt).wait_recv()
-            ms = [rs[k, 0:1, :] for k in range(2 * tp)]
-            top = ms[0]
-            for k in range(1, 2 * tp):
-                top = jnp.maximum(top, ms[k])
-            s = jnp.zeros((1, LANES), f32)
-            w = s
-            p = s
-            for k in range(2 * tp):
-                dm = ms[k] - top
-                f = jnp.exp(dm)
-                s = s + f * rs[k, 1:2, :]
-                w = w + f * (rs[k, 2:3, :] + dm * rs[k, 1:2, :])
-                p = p + rs[k, 3:4, :]
-            log_sum = jnp.log(s)
-            log_norm = top + log_sum
-            ent = log_sum - w / s
-            logp = p - log_norm
-            for k in range(pos):
-                out[k:k + 1, :] = log_norm[:, k * batch:(k + 1) * batch]
-                out[pos + k:pos + k + 1, :] = ent[:, k * batch:(k + 1) * batch]
-                out[2 * pos + k:2 * pos + k + 1, :] = logp[:, k * batch:(k + 1) * batch]
-            for pd, pt, dy, k in peers:
-                s_copy(pd, pt, dy, k, slot).wait_send()
+            with jax.named_scope('combine'):
+                ms = [rs[k, 0:1, :] for k in range(2 * tp)]
+                top = ms[0]
+                for k in range(1, 2 * tp):
+                    top = jnp.maximum(top, ms[k])
+                s = jnp.zeros((1, LANES), f32)
+                w = s
+                p = s
+                for k in range(2 * tp):
+                    dm = ms[k] - top
+                    f = jnp.exp(dm)
+                    s = s + f * rs[k, 1:2, :]
+                    w = w + f * (rs[k, 2:3, :] + dm * rs[k, 1:2, :])
+                    p = p + rs[k, 3:4, :]
+                log_sum = jnp.log(s)
+                log_norm = top + log_sum
+                ent = log_sum - w / s
+                logp = p - log_norm
+                for k in range(pos):
+                    out[k:k + 1, :] = log_norm[:, k * batch:(k + 1) * batch]
+                    out[pos + k:pos + k + 1, :] = ent[:, k * batch:(k + 1) * batch]
+                    out[2 * pos + k:2 * pos + k + 1, :] = logp[:, k * batch:(k + 1) * batch]
+            with jax.named_scope('wsend'):
+                every = rs.at[pl.ds(0, len(peers))]
+                pltpu.make_async_remote_copy(
+                    src_ref=every, dst_ref=every, send_sem=ssem, recv_sem=irecv, device_id=sib, device_id_type=MESH).wait_send()
 
         hbm = pl.BlockSpec(memory_space=pl.ANY)
         vmem = pl.BlockSpec(memory_space=pltpu.VMEM)
@@ -386,7 +362,7 @@
         bf16 = jnp.bfloat16
         packed = pl.pallas_call(
             kernel,
-            out_shape=jax.ShapeDtypeStruct((3 * pos, batch), f32),
+            out_shape=pltpu.VMEM((3 * pos, batch), f32),
             in_specs=[hbm] * 4,
             out_specs=vmem,
             scratch_shapes=[
@@ -406,12 +382,12 @@
                 dma((chunks,)),
                 dma((tiles,)),
                 dma((3,)),
-                dma((parts,)), dma((parts,)),
-                dma((parts,)), dma((parts,)),
-                dma((parts,)), dma((parts,)),
-                dma((parts,)), dma((parts,)),
+                dma, dma((parts,)),
+                dma, dma((parts,)),
+                dma, dma((parts,)),
+                dma, dma((parts,)),
                 dma, dma,
-                dma((2 * tp,)), dma((2 * tp,)),
+                dma, dma((2 * tp,)),
             ],
             compiler_params=pltpu.CompilerParams(
                 collective_id=0, has_side_effects=True, vmem_limit_bytes=60 * 1024 * 1024),
@@ -428,7 +404,7 @@
                        jax.ShapeDtypeStruct((pos, batch), f32)],
             in_specs=[vmem],
             out_specs=[vmem] * 3,
-        )(packed)
+        )(pltpu.with_memory_space_constraint(packed, pltpu.VMEM))
         return logp.T, logn.T, ent.T
 
     specs_in = (P('dp', None, None), P('dp', None), P(None), P(None, 'tp'))

time: 31.6 us -> 28.6 us (0.905)
  Pallas kernels: 30.8 us -> 27.9 us
    pallas_call x1, Pallas kernels: 29.5 us -> 27.3 us  [per_device(): pl.pallas_call(kernel, out_shape=pltpu.VMEM((3 * pos, batch), f32), in_sp...]
    pallas_call x1, Pallas kernels: 1.3 us -> 0.6 us  [per_device(): pl.pallas_call(split, out_shape=[jax.ShapeDtypeStruct((drafts, batch), f3...]
where the time goes in v4:
time: 28.6 us; the launch traced here: 28.5 us
  Pallas kernels  27.9 us (98%)
  between operations  0.64 us (2%)
    pallas_call x1, Pallas kernels, per_device(): pl.pallas_call(kernel, out_shape=pltpu.VMEM((3 * pos, batch), f32), in_sp...  27.3 us
    pallas_call x1, Pallas kernels, per_device(): pl.pallas_call(split, out_shape=[jax.ShapeDtypeStruct((drafts, batch), f3...  0.6 us

profile of v4, /device:TPU:0, one launch (start us, length us, event | category | flops | bytes accessed | tf_op | source)
XLA Modules:
  0.0 28.5 jit_solution(4877612186427218068)
XLA Ops:
  0.6 27.3 %shard_map.67.src = f32[15,16]{1,0:T(8,128)S(1)} custom-call(bf16[80,5120]{1,0:T(8,128)(2,1)} %bitcast.9, s32[4,16]{1,0:T(4,128)} %bitcast.11, bf16[40,128]{1,0:T(8,128)(2,1)} %bitcast.10, bf16[8000,5120]{1,0:T(8,128)(2,1)} %bitcast.4.w_hbm), custom_call_target="tpu_custom_call" | custom-call | tf_op jit(solution)/shard_map/pallas_call | solution.py:363
  27.9 0.6 %shard_map.68 = (f32[4,16]{1,0:T(4,128)}, f32[5,16]{1,0:T(8,128)}, f32[5,16]{1,0:T(8,128)}) custom-call(f32[15,16]{1,0:T(8,128)S(1)} %shard_map.67.src), custom_call_target="tpu_custom_call" | custom-call | tf_op jit(solution)/shard_map/pallas_call | solution.py:401

commit v5 on v4

v5 whole, which is shorter than its diff:
```python
import jax
import jax.numpy as jnp
from jax import lax
from jax.experimental import pallas as pl
from jax.experimental.pallas import tpu as pltpu
from jax.sharding import PartitionSpec as P

NORM_EPS = 1e-5
MESH = pl.DeviceIdType.MESH
LANES = 128
TILE = 256
BLOCK = 800
OWN = 1600
FIRST = 160
CHUNK = 360
LAST = 320
DIRECT = 6
SHARED = 2
OWN_FORWARDS = ((), (0,), (1,), (2, 3))
STEPS = (
    ((), (), ('y0', 'y1', 'a0')),
    ((4, 5), (0,), ('a1', 'y2')),
    ((6,), (1,), ('x0', 'a2')),
    ((7,), (2, 3), ('y3', 'x1', 'b0')),
    ((8, 9), (4, 5), ('a3', 'b1', 'y4', 'x2')),
    ((10, 11), (6, 7), ('a4', 'b2', 'y5', 'x3')),
    ((), (), ('a5', 'b3')),
)
NT = (((1,), (1,)), ((), ()))


def update_stats(z, want, carry, first=None):
    z3 = z.reshape(-1, 8, z.shape[-1])
    bm = jnp.max(z3, axis=0)
    m, s, w, p = carry
    for g in range(z3.shape[0]):
        p = jnp.where(want == g, z3[g], p)
    if m is None:
        sh = z3 - bm[None]
        e = jnp.exp(sh)
        return bm, jnp.sum(e, axis=0), jnp.sum(e * sh, axis=0), p
    mn = jnp.maximum(m, bm)
    dm = m - mn
    a = jnp.exp(dm)
    sh = z3 - mn[None]
    e = jnp.exp(sh)
    w = a * (w + dm * s) + jnp.sum(e * sh, axis=0)
    s = a * s + jnp.sum(e, axis=0)
    return mn, s, w, p


def merge_stats(a, b):
    top = jnp.maximum(a[0], b[0])
    da, db = a[0] - top, b[0] - top
    fa, fb = jnp.exp(da), jnp.exp(db)
    return (
        top,
        fa * a[1] + fb * b[1],
        fa * (a[2] + da * a[1]) + fb * (b[2] + db * b[1]),
        a[3] + b[3],
    )


def keep_row(carry, ids):
    m, s, w, p = carry
    sub = lax.broadcasted_iota(jnp.int32, p.shape, 0)
    return m, s, w, jnp.where(sub == jnp.bitwise_and(ids, 7), p, 0.0)


def pack_stats(carry):
    m, s, w, p = carry
    top = jnp.max(m, axis=0, keepdims=True)
    dm = m - top
    f = jnp.exp(dm)
    return (
        top,
        jnp.sum(f * s, axis=0, keepdims=True),
        jnp.sum(f * (w + dm * s), axis=0, keepdims=True),
        jnp.sum(p, axis=0, keepdims=True),
    )


def solution(mesh):
    tp = mesh.shape['tp']

    def per_device(hidden, draft_ids, norm_gain, head_w):
        batch, pos, dim = hidden.shape
        drafts = draft_ids.shape[1]
        cols = head_w.shape[1]
        half = (cols - OWN) // 2
        chunks = (OWN - FIRST) // CHUNK
        rows = batch * pos
        kblocks = dim // LANES
        tiles = dim // TILE
        unique = DIRECT - SHARED
        assert tiles == tp * unique + 2 * SHARED
        parts = 2 * DIRECT
        crossing = 2 * unique
        nblocks = half // BLOCK
        f32 = jnp.float32

        def kernel(x_hbm, ids_hbm, g_hbm, w_hbm, out,
                   hv, ev, wv, xv, nb, nf, pf, acc, gv, gf, idv, idp, st, rs,
                   esem, wsem, lsem, ysend, yrecv, xsend, xrecv, asend, arecv, bsend, brecv, isend, irecv, ssem, rsem):
            t = lax.axis_index('tp')
            d = lax.axis_index('dp')
            y = lax.rem(d, 2)
            core = lax.rem(t, 2)
            mate = (d + 1 - 2 * y, t)
            sib = (d, t + 1 - 2 * core)
            nbr_t = lax.rem(t + 2, tp)
            nbr = (d, nbr_t)
            sib_t = t + 1 - 2 * core
            far_t = lax.rem(sib_t + 2, tp)

            cx = pltpu.make_async_copy(x_hbm, xv, lsem.at[0])
            cg = pltpu.make_async_copy(g_hbm, gv, lsem.at[1])
            ci = pltpu.make_async_copy(ids_hbm, idv, lsem.at[2])
            cg.start()
            ci.start()
            for k in range(pos):
                part = pl.ds(k * batch, batch)
                pltpu.make_async_copy(x_hbm.at[part], xv.at[part], lsem.at[0]).start()

            def w_copy(kt, group):
                return pltpu.make_async_copy(
                    w_hbm.at[pl.ds(pl.multiple_of(OWN + y * half, 16), half), pl.ds(pl.multiple_of(kt * TILE, TILE), TILE)],
                    wv.at[kt], wsem.at[group])

            def w_start(group):
                for name in STEPS[group][2]:
                    w_copy(kt_of(name), group).start()

            def w_wait(group):
                some = wv.at[pl.ds(0, len(STEPS[group][2]))]
                pltpu.make_async_copy(some, some, wsem.at[group]).wait()

            def tile_of(owner, i):
                if i < unique:
                    return owner * unique + i
                return tp * unique + lax.rem(owner, 2) * SHARED + i - unique

            def block_of(owner, i):
                return 2 * tile_of(owner, i // 2) + i % 2

            stream_t = {'y': t, 'a': sib_t, 'x': nbr_t, 'b': far_t}

            def kt_of(name):
                return tile_of(stream_t[name[0]], int(name[1:]))

            def e_copy(e):
                return pltpu.make_async_copy(
                    w_hbm.at[pl.ds(pl.multiple_of(FIRST + e * CHUNK, 8), CHUNK), :], ev.at[e], esem.at[lax.rem(e, 2)])

            head_copy = pltpu.make_async_copy(w_hbm.at[pl.ds(0, FIRST), :], hv, lsem.at[3])
            head_copy.start()
            e_copy(0).start()
            barrier = pltpu.get_barrier_semaphore()
            peers = []
            for dy in range(2):
                for k in range(tp):
                    if dy or k:
                        peers.append((mate[0] if dy else d, lax.rem(t + k, tp), dy, k))
            for near in (mate, sib, nbr):
                pl.semaphore_signal(barrier, inc=1, device_id=near, device_id_type=MESH)

            def y_copy(i):
                return pltpu.make_async_remote_copy(
                    src_ref=nf.at[i], dst_ref=pf.at[block_of(t, i)], send_sem=ysend, recv_sem=yrecv.at[i],
                    device_id=mate, device_id_type=MESH)

            def x_copy(i, owner):
                kb = block_of(owner, i)
                return pltpu.make_async_remote_copy(
                    src_ref=pf.at[kb], dst_ref=pf.at[kb], send_sem=xsend, recv_sem=xrecv.at[i],
                    device_id=nbr, device_id_type=MESH)

            def a_copy(i, owner):
                kb = block_of(owner, i)
                return pltpu.make_async_remote_copy(
                    src_ref=pf.at[kb], dst_ref=pf.at[kb], send_sem=asend, recv_sem=arecv.at[i // 2],
                    device_id=sib, device_id_type=MESH)

            def b_copy(i, owner):
                kb = block_of(owner, i)
                return pltpu.make_async_remote_copy(
                    src_ref=pf.at[kb], dst_ref=pf.at[kb], send_sem=bsend, recv_sem=brecv.at[i // 2],
                    device_id=sib, device_id_type=MESH)

            def tile_recv(owner, i, send, recv):
                both = pf.at[pl.ds(2 * tile_of(owner, i), 2)]
                pltpu.make_async_remote_copy(
                    src_ref=both, dst_ref=both, send_sem=send, recv_sem=recv.at[i],
                    device_id=sib, device_id_type=MESH).wait_recv()

            id_copy = pltpu.make_async_remote_copy(
                src_ref=idv, dst_ref=idp, send_sem=isend, recv_sem=irecv, device_id=mate, device_id_type=MESH)

            nb[rows:LANES, :] = jnp.zeros((LANES - rows, dim), jnp.bfloat16)
            nb[LANES + rows:, :] = jnp.zeros((LANES - rows, dim), jnp.bfloat16)
            with jax.named_scope('waitg'):
                ci.wait()
                cg.wait()
            gf[...] = gv[...].astype(f32)
            with jax.named_scope('waitx'):
                cx.wait()
            sq = jnp.zeros((rows, LANES), f32)
            for k in range(kblocks):
                x = xv[:, k * LANES:(k + 1) * LANES].astype(f32)
                sq = sq + x * x
            inv = lax.rsqrt(jnp.sum(sq, axis=1, keepdims=True) / dim + NORM_EPS)

            def normed(kb):
                x = xv[:, pl.ds(pl.multiple_of(kb * LANES, LANES), LANES)].astype(f32)
                return (x * inv * gf[pl.ds(kb, 1), :]).astype(jnp.bfloat16)

            for i in range(parts):
                nf[i] = normed(block_of(t, i)).astype(f32)
            with jax.named_scope('barr'):
                pl.semaphore_wait(barrier, 3)
            for i in range(parts):
                y_copy(i).start()
            id_copy.start()
            for k in range(kblocks):
                nb[:rows, k * LANES:(k + 1) * LANES] = normed(k)

            def forward_y(i):
                y_copy(i).wait_recv()
                if i < crossing:
                    x_copy(i, t).start()
                a_copy(i, t).start()

            def forward_x(i):
                x_copy(i, nbr_t).wait_recv()
                b_copy(i, nbr_t).start()

            def load_tile(name):
                kt = kt_of(name)
                i = int(name[1:])
                with jax.named_scope('wait_' + name):
                    if name[0] == 'a':
                        tile_recv(sib_t, i, asend, arecv)
                    if name[0] == 'b':
                        tile_recv(far_t, i, bsend, brecv)
                for h in range(2):
                    nb[LANES:LANES + rows, pl.ds(pl.multiple_of(kt * TILE + h * LANES, LANES), LANES)] = (
                        pf[2 * kt + h].astype(jnp.bfloat16))

            def tiles_dot(names, r):
                z = None
                for name in names:
                    kt = kt_of(name)
                    one = lax.dot_general(wv[kt, r, :], nb[:, pl.ds(pl.multiple_of(kt * TILE, TILE), TILE)], NT,
                                          preferred_element_type=f32)
                    z = one if z is None else z + one
                return z

            pad = jnp.full((1, LANES - drafts * batch), -8, jnp.int32)
            own_ids = jnp.concatenate([idv[k:k + 1, :] - t * cols for k in range(drafts)] + [pad], axis=1)
            own_want = jnp.broadcast_to(jnp.right_shift(own_ids, 3), (8, LANES))
            zero = jnp.zeros((8, LANES), f32)

            def own_forward(e):
                for chunk, blocks in enumerate(OWN_FORWARDS):
                    if blocks:
                        @pl.when(e == chunk)
                        def _():
                            with jax.named_scope('fy'):
                                for i in blocks:
                                    forward_y(i)

            with jax.named_scope('waite'):
                head_copy.wait()
            e_copy(1).start()
            with jax.named_scope('own'):
                z = lax.dot_general(hv[...], nb[:LANES, :], NT, preferred_element_type=f32)
                own_carry = update_stats(z, own_want, (None, None, None, zero))

            def own_step(e, carry):
                with jax.named_scope('waite'):
                    e_copy(e).wait()

                @pl.when(e + 2 < chunks)
                def _():
                    e_copy(e + 2).start()

                for chunk, groups in ((2, (0,)), (3, (1, 2))):
                    @pl.when(e == chunk)
                    def _():
                        for group in groups:
                            w_start(group)

                with jax.named_scope('own'):
                    z = lax.dot_general(ev[e], nb[:LANES, :], NT, preferred_element_type=f32)
                    carry = update_stats(z, own_want - (FIRST + e * CHUNK) // 8, carry)
                own_forward(e)
                return carry

            own_carry = lax.fori_loop(0, chunks, own_step, own_carry)
            own_carry = keep_row(own_carry, own_ids)

            for n_step, (ys, xs, names) in enumerate(STEPS[:-1]):
                for i in ys:
                    with jax.named_scope('fy'):
                        forward_y(i)
                for i in xs:
                    with jax.named_scope('fx'):
                        forward_x(i)
                for name in names:
                    load_tile(name)
                with jax.named_scope('ww'):
                    w_wait(n_step)
                if n_step + 3 < len(STEPS):
                    w_start(n_step + 3)

                @pl.when(t >= 0)
                def _():
                    with jax.named_scope('step'):
                        for n in range(nblocks):
                            r = slice(n * BLOCK, (n + 1) * BLOCK)
                            z = tiles_dot(names, r)
                            acc[r, :] = z if n_step == 0 else acc[r, :] + z

            id_copy.wait_recv()
            base = t * cols + OWN + y * half
            ids = jnp.concatenate([idv[k:k + 1, :] - base for k in range(drafts)] + [pad]
                                  + [idp[k:k + 1, :] - base for k in range(drafts)] + [pad], axis=1)
            want = jnp.broadcast_to(jnp.right_shift(ids, 3), (8, 2 * LANES))
            for name in STEPS[-1][2]:
                load_tile(name)
            with jax.named_scope('ww'):
                w_wait(len(STEPS) - 1)
            carry = (None, None, None, jnp.zeros((8, 2 * LANES), f32))
            with jax.named_scope('final'):
                for n in range(half // LAST):
                    r = slice(n * LAST, (n + 1) * LAST)
                    z = acc[r, :] + tiles_dot(STEPS[-1][2], r)
                    carry = update_stats(z, want - n * LAST // 8, carry)
            carry = keep_row(carry, ids)
            mine = pack_stats(merge_stats(own_carry, [c[:, :LANES] for c in carry]))
            theirs = pack_stats([c[:, LANES:] for c in carry])
            slot = y * tp + t
            for k in range(4):
                st[0, k:k + 1, :] = mine[k]
                st[1, k:k + 1, :] = theirs[k]
                rs[slot, k:k + 1, :] = mine[k]

            def s_copy(pd, pt, dy, k, into):
                return pltpu.make_async_remote_copy(
                    src_ref=st.at[dy], dst_ref=rs.at[into], send_sem=ssem, recv_sem=rsem,
                    device_id=(pd, pt), device_id_type=MESH)

            for pd, pt, dy, k in peers:
                s_copy(pd, pt, dy, k, slot).start()
            for sem, count in ((ysend, parts), (xsend, crossing), (asend, parts), (bsend, crossing)):
                sent = nf.at[pl.ds(0, count)]
                pltpu.make_async_remote_copy(
                    src_ref=sent, dst_ref=sent, send_sem=sem, recv_sem=irecv, device_id=sib, device_id_type=MESH).wait_send()
            id_copy.wait_send()
            with jax.named_scope('wstat'):
                every = rs.at[pl.ds(0, len(peers))]
                stats_copy = pltpu.make_async_remote_copy(
                    src_ref=every, dst_ref=every, send_sem=ssem, recv_sem=rsem, device_id=sib, device_id_type=MESH)
                stats_copy.wait_recv()
            with jax.named_scope('combine'):
                ms = [rs[k, 0:1, :] for k in range(2 * tp)]
                top = ms[0]
                for k in range(1, 2 * tp):
                    top = jnp.maximum(top, ms[k])
                s = jnp.zeros((1, LANES), f32)
                w = s
                p = s
                for k in range(2 * tp):
                    dm = ms[k] - top
                    f = jnp.exp(dm)
                    s = s + f * rs[k, 1:2, :]
                    w = w + f * (rs[k, 2:3, :] + dm * rs[k, 1:2, :])
                    p = p + rs[k, 3:4, :]
                log_sum = jnp.log(s)
                log_norm = top + log_sum
                ent = log_sum - w / s
                logp = p - log_norm
                for k in range(pos):
                    out[k:k + 1, :] = log_norm[:, k * batch:(k + 1) * batch]
                    out[pos + k:pos + k + 1, :] = ent[:, k * batch:(k + 1) * batch]
                    out[2 * pos + k:2 * pos + k + 1, :] = logp[:, k * batch:(k + 1) * batch]
            with jax.named_scope('wsend'):
                stats_copy.wait_send()

        hbm = pl.BlockSpec(memory_space=pl.ANY)
        vmem = pl.BlockSpec(memory_space=pltpu.VMEM)
        dma = pltpu.SemaphoreType.DMA
        bf16 = jnp.bfloat16
        packed = pl.pallas_call(
            kernel,
            out_shape=pltpu.VMEM((3 * pos, batch), f32),
            in_specs=[hbm] * 4,
            out_specs=vmem,
            scratch_shapes=[
                pltpu.VMEM((FIRST, dim), bf16),
                pltpu.VMEM((chunks, CHUNK, dim), bf16),
                pltpu.VMEM((tiles, half, TILE), bf16),
                pltpu.VMEM((rows, dim), bf16),
                pltpu.VMEM((2 * LANES, dim), bf16),
                pltpu.VMEM((parts, rows, LANES), f32),
                pltpu.VMEM((kblocks, rows, LANES), f32),
                pltpu.VMEM((half, 2 * LANES), f32),
                pltpu.VMEM((kblocks, LANES), bf16),
                pltpu.VMEM((kblocks, LANES), f32),
                pltpu.VMEM((drafts, batch), jnp.int32),
                pltpu.VMEM((drafts, batch), jnp.int32),
                pltpu.VMEM((2, 8, LANES), f32),
                pltpu.VMEM((2 * tp, 8, LANES), f32),
                dma((2,)),
                dma((len(STEPS),)),
                dma((4,)),
                dma, dma((parts,)),
                dma, dma((crossing,)),
                dma, dma((DIRECT,)),
                dma, dma((unique,)),
                dma, dma,
                dma, dma,
            ],
            compiler_params=pltpu.CompilerParams(
                collective_id=0, has_side_effects=True, vmem_limit_bytes=60 * 1024 * 1024),
        )(hidden.transpose(1, 0, 2).reshape(rows, dim), draft_ids.T, norm_gain.reshape(kblocks, LANES), head_w.T)

        def split(src, o_logp, o_logn, o_ent):
            o_logn[...] = src[:pos, :]
            o_ent[...] = src[pos:2 * pos, :]
            o_logp[...] = src[2 * pos:2 * pos + drafts, :]

        logp, logn, ent = pl.pallas_call(
            split,
            out_shape=[jax.ShapeDtypeStruct((drafts, batch), f32), jax.ShapeDtypeStruct((pos, batch), f32),
                       jax.ShapeDtypeStruct((pos, batch), f32)],
            in_specs=[vmem],
            out_specs=[vmem] * 3,
        )(pltpu.with_memory_space_constraint(packed, pltpu.VMEM))
        return logp.T, logn.T, ent.T

    specs_in = (P('dp', None, None), P('dp', None), P(None), P(None, 'tp'))
    specs_out = (P('dp', None), P('dp', None), P('dp', None))
    return jax.shard_map(per_device, mesh=mesh, in_specs=specs_in, out_specs=specs_out, check_vma=False)
```

time: 28.6 us -> 27.9 us (0.976)
  Pallas kernels: 27.9 us -> 27.1 us
    pallas_call x1, Pallas kernels: 27.3 us -> 26.5 us  [per_device(): pl.pallas_call(kernel, out_shape=pltpu.VMEM((3 * pos, batch), f32), in_sp...]
where the time goes in v5:
time: 27.9 us; the launch traced here: 27.8 us
  Pallas kernels  27.1 us (97%)
  between operations  0.64 us (2%)
    pallas_call x1, Pallas kernels, per_device(): pl.pallas_call(kernel, out_shape=pltpu.VMEM((3 * pos, batch), f32), in_sp...  26.5 us
    pallas_call x1, Pallas kernels, per_device(): pl.pallas_call(split, out_shape=[jax.ShapeDtypeStruct((drafts, batch), f3...  0.6 us

profile of v5, /device:TPU:0, one launch (start us, length us, event | category | flops | bytes accessed | tf_op | source)
XLA Modules:
  0.0 27.8 jit_solution(1634023400533431260)
XLA Ops:
  0.6 26.5 %shard_map.67.src = f32[15,16]{1,0:T(8,128)S(1)} custom-call(bf16[80,5120]{1,0:T(8,128)(2,1)} %bitcast.9, s32[4,16]{1,0:T(4,128)} %bitcast.11, bf16[40,128]{1,0:T(8,128)(2,1)} %bitcast.10, bf16[8000,5120]{1,0:T(8,128)(2,1)} %bitcast.4.w_hbm), custom_call_target="tpu_custom_call" | custom-call | tf_op jit(solution)/shard_map/pallas_call | solution.py:394
  27.2 0.6 %shard_map.68 = (f32[4,16]{1,0:T(4,128)}, f32[5,16]{1,0:T(8,128)}, f32[5,16]{1,0:T(8,128)}) custom-call(f32[15,16]{1,0:T(8,128)S(1)} %shard_map.67.src), custom_call_target="tpu_custom_call" | custom-call | tf_op jit(solution)/shard_map/pallas_call | solution.py:433

commit v6 on v5

--- a/solution.py
+++ b/solution.py
@@ -198,10 +198,6 @@
 
             nb[rows:LANES, :] = jnp.zeros((LANES - rows, dim), jnp.bfloat16)
             nb[LANES + rows:, :] = jnp.zeros((LANES - rows, dim), jnp.bfloat16)
-            with jax.named_scope('waitg'):
-                ci.wait()
-                cg.wait()
-            gf[...] = gv[...].astype(f32)
             with jax.named_scope('waitx'):
                 cx.wait()
             sq = jnp.zeros((rows, LANES), f32)
@@ -210,12 +206,18 @@
                 sq = sq + x * x
             inv = lax.rsqrt(jnp.sum(sq, axis=1, keepdims=True) / dim + NORM_EPS)
 
+            with jax.named_scope('waitg'):
+                ci.wait()
+                cg.wait()
+            gf[...] = gv[...].astype(f32)
+
             def normed(kb):
                 x = xv[:, pl.ds(pl.multiple_of(kb * LANES, LANES), LANES)].astype(f32)
                 return (x * inv * gf[pl.ds(kb, 1), :]).astype(jnp.bfloat16)
 
             for i in range(parts):
                 nf[i] = normed(block_of(t, i)).astype(f32)
+            e_copy(1).start()
             with jax.named_scope('barr'):
                 pl.semaphore_wait(barrier, 3)
             for i in range(parts):
@@ -271,7 +273,6 @@
 
             with jax.named_scope('waite'):
                 head_copy.wait()
-            e_copy(1).start()
             with jax.named_scope('own'):
                 z = lax.dot_general(hv[...], nb[:LANES, :], NT, preferred_element_type=f32)
                 own_carry = update_stats(z, own_want, (None, None, None, zero))

time: 27.9 us -> 27.9 us (level)
  no operation moved by 1% of the time
where the time goes in v6:
time: 27.9 us; the launch traced here: 27.8 us
  Pallas kernels  27.1 us (97%)
  between operations  0.64 us (2%)
    pallas_call x1, Pallas kernels, per_device(): pl.pallas_call(kernel, out_shape=pltpu.VMEM((3 * pos, batch), f32), in_sp...  26.5 us
    pallas_call x1, Pallas kernels, per_device(): pl.pallas_call(split, out_shape=[jax.ShapeDtypeStruct((drafts, batch), f3...  0.6 us

profile of v6, /device:TPU:0, one launch (start us, length us, event | category | flops | bytes accessed | tf_op | source)
XLA Modules:
  0.0 27.8 jit_solution(5299932485934781018)
XLA Ops:
  0.6 26.5 %shard_map.67.src = f32[15,16]{1,0:T(8,128)S(1)} custom-call(bf16[80,5120]{1,0:T(8,128)(2,1)} %bitcast.9, s32[4,16]{1,0:T(4,128)} %bitcast.11, bf16[40,128]{1,0:T(8,128)(2,1)} %bitcast.10, bf16[8000,5120]{1,0:T(8,128)(2,1)} %bitcast.4.w_hbm), custom_call_target="tpu_custom_call" | custom-call | tf_op jit(solution)/shard_map/pallas_call | solution.py:395
  27.2 0.6 %shard_map.68 = (f32[4,16]{1,0:T(4,128)}, f32[5,16]{1,0:T(8,128)}, f32[5,16]{1,0:T(8,128)}) custom-call(f32[15,16]{1,0:T(8,128)S(1)} %shard_map.67.src), custom_call_target="tpu_custom_call" | custom-call | tf_op jit(solution)/shard_map/pallas_call | solution.py:434

commit v7 on v6

--- a/solution.py
+++ b/solution.py
@@ -292,6 +292,7 @@
                             w_start(group)
 
                 with jax.named_scope('own'):
+                    pl.delay(1)
                     z = lax.dot_general(ev[e], nb[:LANES, :], NT, preferred_element_type=f32)
                     carry = update_stats(z, own_want - (FIRST + e * CHUNK) // 8, carry)
                 own_forward(e)

time: 27.9 us -> 26.8 us (0.961)
  Pallas kernels: 27.1 us -> 26.1 us
    pallas_call x1, Pallas kernels: 26.5 us -> 25.5 us  [per_device(): pl.pallas_call(kernel, out_shape=pltpu.VMEM((3 * pos, batch), f32), in_sp...]
where the time goes in v7:
time: 26.8 us; the launch traced here: 26.7 us
  Pallas kernels  26.1 us (97%)
  between operations  0.64 us (2%)
    pallas_call x1, Pallas kernels, per_device(): pl.pallas_call(kernel, out_shape=pltpu.VMEM((3 * pos, batch), f32), in_sp...  25.5 us
    pallas_call x1, Pallas kernels, per_device(): pl.pallas_call(split, out_shape=[jax.ShapeDtypeStruct((drafts, batch), f3...  0.6 us

profile of v7, /device:TPU:0, one launch (start us, length us, event | category | flops | bytes accessed | tf_op | source)
XLA Modules:
  0.0 26.7 jit_solution(708007795520179432)
XLA Ops:
  0.6 25.5 %shard_map.67.src = f32[15,16]{1,0:T(8,128)S(1)} custom-call(bf16[80,5120]{1,0:T(8,128)(2,1)} %bitcast.9, s32[4,16]{1,0:T(4,128)} %bitcast.11, bf16[40,128]{1,0:T(8,128)(2,1)} %bitcast.10, bf16[8000,5120]{1,0:T(8,128)(2,1)} %bitcast.4.w_hbm), custom_call_target="tpu_custom_call" | custom-call | tf_op jit(solution)/shard_map/pallas_call | solution.py:396
  26.1 0.6 %shard_map.68 = (f32[4,16]{1,0:T(4,128)}, f32[5,16]{1,0:T(8,128)}, f32[5,16]{1,0:T(8,128)}) custom-call(f32[15,16]{1,0:T(8,128)S(1)} %shard_map.67.src), custom_call_target="tpu_custom_call" | custom-call | tf_op jit(solution)/shard_map/pallas_call | solution.py:435

commit v8 on v7

--- a/solution.py
+++ b/solution.py
@@ -11,21 +11,32 @@
 TILE = 256
 BLOCK = 800
 OWN = 1600
-FIRST = 160
-CHUNK = 360
+FIRST = 400
+CHUNK = 400
 LAST = 320
 DIRECT = 6
 SHARED = 2
-OWN_FORWARDS = ((), (0,), (1,), (2, 3))
+OWN_FORWARDS = ((0,), (1, 2), (3,))
 STEPS = (
-    ((), (), ('y0', 'y1', 'a0')),
-    ((4, 5), (0,), ('a1', 'y2')),
-    ((6,), (1,), ('x0', 'a2')),
-    ((7,), (2, 3), ('y3', 'x1', 'b0')),
+    ((), (), ('y0', 'a0', 'y1')),
+    ((4, 5), (0, 1), ('a1', 'y2', 'x0')),
+    ((6, 7), (2, 3), ('a2', 'b0', 'y3', 'x1')),
     ((8, 9), (4, 5), ('a3', 'b1', 'y4', 'x2')),
-    ((10, 11), (6, 7), ('a4', 'b2', 'y5', 'x3')),
-    ((), (), ('a5', 'b3')),
+    ((10, 11), (6, 7), ('a4', 'b2')),
+    ((), (), ('y5', 'x3', 'a5', 'b3')),
 )
+Y_GROUPS = tuple(g for g in OWN_FORWARDS + tuple(ys for ys, _, _ in STEPS) if g)
+X_GROUPS = tuple(xs for _, xs, _ in STEPS if xs)
+
+
+def group_of(groups, i):
+    return [i in g for g in groups].index(True)
+
+
+def step_of(kind, i):
+    return [kind + str(i) in names for _, _, names in STEPS].index(True)
+
+
 NT = (((1,), (1,)), ((), ()))
 
 
@@ -96,12 +107,13 @@
         assert tiles == tp * unique + 2 * SHARED
         parts = 2 * DIRECT
         crossing = 2 * unique
+        assert 2 * (parts + crossing) == kblocks
         nblocks = half // BLOCK
         f32 = jnp.float32
 
         def kernel(x_hbm, ids_hbm, g_hbm, w_hbm, out,
                    hv, ev, wv, xv, nb, nf, pf, acc, gv, gf, idv, idp, st, rs,
-                   esem, wsem, lsem, ysend, yrecv, xsend, xrecv, asend, arecv, bsend, brecv, isend, irecv, ssem, rsem):
+                   esem, wsem, lsem, psend, yrecv, xrecv, srecv, isend, irecv, ssem, rsem):
             t = lax.axis_index('tp')
             d = lax.axis_index('dp')
             y = lax.rem(d, 2)
@@ -166,31 +178,31 @@
 
             def y_copy(i):
                 return pltpu.make_async_remote_copy(
-                    src_ref=nf.at[i], dst_ref=pf.at[block_of(t, i)], send_sem=ysend, recv_sem=yrecv.at[i],
+                    src_ref=nf.at[i], dst_ref=pf.at[block_of(t, i)], send_sem=psend, recv_sem=yrecv.at[group_of(Y_GROUPS, i)],
                     device_id=mate, device_id_type=MESH)
 
             def x_copy(i, owner):
                 kb = block_of(owner, i)
                 return pltpu.make_async_remote_copy(
-                    src_ref=pf.at[kb], dst_ref=pf.at[kb], send_sem=xsend, recv_sem=xrecv.at[i],
+                    src_ref=pf.at[kb], dst_ref=pf.at[kb], send_sem=psend, recv_sem=xrecv.at[group_of(X_GROUPS, i)],
                     device_id=nbr, device_id_type=MESH)
 
             def a_copy(i, owner):
                 kb = block_of(owner, i)
                 return pltpu.make_async_remote_copy(
-                    src_ref=pf.at[kb], dst_ref=pf.at[kb], send_sem=asend, recv_sem=arecv.at[i // 2],
+                    src_ref=pf.at[kb], dst_ref=pf.at[kb], send_sem=psend, recv_sem=srecv.at[step_of('a', i // 2)],
                     device_id=sib, device_id_type=MESH)
 
             def b_copy(i, owner):
                 kb = block_of(owner, i)
                 return pltpu.make_async_remote_copy(
-                    src_ref=pf.at[kb], dst_ref=pf.at[kb], send_sem=bsend, recv_sem=brecv.at[i // 2],
+                    src_ref=pf.at[kb], dst_ref=pf.at[kb], send_sem=psend, recv_sem=srecv.at[step_of('b', i // 2)],
                     device_id=sib, device_id_type=MESH)
 
-            def tile_recv(owner, i, send, recv):
-                both = pf.at[pl.ds(2 * tile_of(owner, i), 2)]
+            def blocks_recv(count, recv):
+                some = pf.at[pl.ds(0, count)]
                 pltpu.make_async_remote_copy(
-                    src_ref=both, dst_ref=both, send_sem=send, recv_sem=recv.at[i],
+                    src_ref=some, dst_ref=some, send_sem=psend, recv_sem=recv,
                     device_id=sib, device_id_type=MESH).wait_recv()
 
             id_copy = pltpu.make_async_remote_copy(
@@ -226,24 +238,27 @@
             for k in range(kblocks):
                 nb[:rows, k * LANES:(k + 1) * LANES] = normed(k)
 
-            def forward_y(i):
-                y_copy(i).wait_recv()
-                if i < crossing:
-                    x_copy(i, t).start()
-                a_copy(i, t).start()
-
-            def forward_x(i):
-                x_copy(i, nbr_t).wait_recv()
-                b_copy(i, nbr_t).start()
+            def forward_y(group):
+                if group:
+                    blocks_recv(len(group), yrecv.at[group_of(Y_GROUPS, group[0])])
+                for i in group:
+                    if i < crossing:
+                        x_copy(i, t).start()
+                    a_copy(i, t).start()
+
+            def forward_x(group):
+                if group:
+                    blocks_recv(len(group), xrecv.at[group_of(X_GROUPS, group[0])])
+                for i in group:
+                    b_copy(i, nbr_t).start()
+
+            def sibling_wait(step):
+                count = len([name for name in STEPS[step][2] if name[0] in 'ab'])
+                if count:
+                    blocks_recv(2 * count, srecv.at[step])
 
             def load_tile(name):
                 kt = kt_of(name)
-                i = int(name[1:])
-                with jax.named_scope('wait_' + name):
-                    if name[0] == 'a':
-                        tile_recv(sib_t, i, asend, arecv)
-                    if name[0] == 'b':
-                        tile_recv(far_t, i, bsend, brecv)
                 for h in range(2):
                     nb[LANES:LANES + rows, pl.ds(pl.multiple_of(kt * TILE + h * LANES, LANES), LANES)] = (
                         pf[2 * kt + h].astype(jnp.bfloat16))
@@ -268,8 +283,7 @@
                         @pl.when(e == chunk)
                         def _():
                             with jax.named_scope('fy'):
-                                for i in blocks:
-                                    forward_y(i)
+                                forward_y(blocks)
 
             with jax.named_scope('waite'):
                 head_copy.wait()
@@ -285,7 +299,7 @@
                 def _():
                     e_copy(e + 2).start()
 
-                for chunk, groups in ((2, (0,)), (3, (1, 2))):
+                for chunk, groups in ((1, (0,)), (2, (1, 2))):
                     @pl.when(e == chunk)
                     def _():
                         for group in groups:
@@ -302,12 +316,12 @@
             own_carry = keep_row(own_carry, own_ids)
 
             for n_step, (ys, xs, names) in enumerate(STEPS[:-1]):
-                for i in ys:
-                    with jax.named_scope('fy'):
-                        forward_y(i)
-                for i in xs:
-                    with jax.named_scope('fx'):
-                        forward_x(i)
+                with jax.named_scope('fy'):
+                    forward_y(ys)
+                with jax.named_scope('fx'):
+                    forward_x(xs)
+                with jax.named_scope('ws'):
+                    sibling_wait(n_step)
                 for name in names:
                     load_tile(name)
                 with jax.named_scope('ww'):
@@ -328,6 +342,7 @@
             ids = jnp.concatenate([idv[k:k + 1, :] - base for k in range(drafts)] + [pad]
                                   + [idp[k:k + 1, :] - base for k in range(drafts)] + [pad], axis=1)
             want = jnp.broadcast_to(jnp.right_shift(ids, 3), (8, 2 * LANES))
+            sibling_wait(len(STEPS) - 1)
             for name in STEPS[-1][2]:
                 load_tile(name)
             with jax.named_scope('ww'):
@@ -354,10 +369,8 @@
 
             for pd, pt, dy, k in peers:
                 s_copy(pd, pt, dy, k, slot).start()
-            for sem, count in ((ysend, parts), (xsend, crossing), (asend, parts), (bsend, crossing)):
-                sent = nf.at[pl.ds(0, count)]
-                pltpu.make_async_remote_copy(
-                    src_ref=sent, dst_ref=sent, send_sem=sem, recv_sem=irecv, device_id=sib, device_id_type=MESH).wait_send()
+            pltpu.make_async_remote_copy(
+                src_ref=pf, dst_ref=pf, send_sem=psend, recv_sem=irecv, device_id=sib, device_id_type=MESH).wait_send()
             id_copy.wait_send()
             with jax.named_scope('wstat'):
                 every = rs.at[pl.ds(0, len(peers))]
@@ -416,10 +429,10 @@
                 dma((2,)),
                 dma((len(STEPS),)),
                 dma((4,)),
-                dma, dma((parts,)),
-                dma, dma((crossing,)),
-                dma, dma((DIRECT,)),
-                dma, dma((unique,)),
+                dma,
+                dma((len(Y_GROUPS),)),
+                dma((len(X_GROUPS),)),
+                dma((len(STEPS),)),
                 dma, dma,
                 dma, dma,
             ],

time: 26.8 us -> 26.4 us (0.985)
  Pallas kernels: 26.1 us -> 25.7 us
    pallas_call x1, Pallas kernels: 25.5 us -> 25.1 us  [per_device(): pl.pallas_call(kernel, out_shape=pltpu.VMEM((3 * pos, batch), f32), in_sp...]
where the time goes in v8:
time: 26.4 us; the launch traced here: 26.3 us
  Pallas kernels  25.7 us (97%)
  between operations  0.64 us (2%)
    pallas_call x1, Pallas kernels, per_device(): pl.pallas_call(kernel, out_shape=pltpu.VMEM((3 * pos, batch), f32), in_sp...  25.1 us
    pallas_call x1, Pallas kernels, per_device(): pl.pallas_call(split, out_shape=[jax.ShapeDtypeStruct((drafts, batch), f3...  0.6 us

profile of v8, /device:TPU:0, one launch (start us, length us, event | category | flops | bytes accessed | tf_op | source)
XLA Modules:
  0.0 26.3 jit_solution(5494067877751121812)
XLA Ops:
  0.6 25.1 %shard_map.67.src = f32[15,16]{1,0:T(8,128)S(1)} custom-call(bf16[80,5120]{1,0:T(8,128)(2,1)} %bitcast.9, s32[4,16]{1,0:T(4,128)} %bitcast.11, bf16[40,128]{1,0:T(8,128)(2,1)} %bitcast.10, bf16[8000,5120]{1,0:T(8,128)(2,1)} %bitcast.4.w_hbm), custom_call_target="tpu_custom_call" | custom-call | tf_op jit(solution)/shard_map/pallas_call | solution.py:409
  25.7 0.6 %shard_map.68 = (f32[4,16]{1,0:T(4,128)}, f32[5,16]{1,0:T(8,128)}, f32[5,16]{1,0:T(8,128)}) custom-call(f32[15,16]{1,0:T(8,128)S(1)} %shard_map.67.src), custom_call_target="tpu_custom_call" | custom-call | tf_op jit(solution)/shard_map/pallas_call | solution.py:448

commit v9 on v8

--- a/solution.py
+++ b/solution.py
@@ -367,7 +367,7 @@
                     src_ref=st.at[dy], dst_ref=rs.at[into], send_sem=ssem, recv_sem=rsem,
                     device_id=(pd, pt), device_id_type=MESH)
 
-            for pd, pt, dy, k in peers:
+            for pd, pt, dy, k in sorted(peers, key=lambda q: -(2 * q[2] + (q[3] >= 2) + (q[3] == 2))):
                 s_copy(pd, pt, dy, k, slot).start()
             pltpu.make_async_remote_copy(
                 src_ref=pf, dst_ref=pf, send_sem=psend, recv_sem=irecv, device_id=sib, device_id_type=MESH).wait_send()

time: 26.4 us -> 26.3 us (level)
  no operation moved by 1% of the time
where the time goes in v9:
time: 26.3 us; the launch traced here: 26.2 us
  Pallas kernels  25.6 us (97%)
  between operations  0.64 us (2%)
    pallas_call x1, Pallas kernels, per_device(): pl.pallas_call(kernel, out_shape=pltpu.VMEM((3 * pos, batch), f32), in_sp...  25 us
    pallas_call x1, Pallas kernels, per_device(): pl.pallas_call(split, out_shape=[jax.ShapeDtypeStruct((drafts, batch), f3...  0.6 us

profile of v9, /device:TPU:0, one launch (start us, length us, event | category | flops | bytes accessed | tf_op | source)
XLA Modules:
  0.0 26.2 jit_solution(11859485972481307871)
XLA Ops:
  0.6 25.0 %shard_map.67.src = f32[15,16]{1,0:T(8,128)S(1)} custom-call(bf16[80,5120]{1,0:T(8,128)(2,1)} %bitcast.9, s32[4,16]{1,0:T(4,128)} %bitcast.11, bf16[40,128]{1,0:T(8,128)(2,1)} %bitcast.10, bf16[8000,5120]{1,0:T(8,128)(2,1)} %bitcast.4.w_hbm), custom_call_target="tpu_custom_call" | custom-call | tf_op jit(solution)/shard_map/pallas_call | solution.py:409
  25.6 0.6 %shard_map.68 = (f32[4,16]{1,0:T(4,128)}, f32[5,16]{1,0:T(8,128)}, f32[5,16]{1,0:T(8,128)}) custom-call(f32[15,16]{1,0:T(8,128)S(1)} %shard_map.67.src), custom_call_target="tpu_custom_call" | custom-call | tf_op jit(solution)/shard_map/pallas_call | solution.py:448

commit v10 on v9

--- a/solution.py
+++ b/solution.py
@@ -128,16 +128,16 @@
             cx = pltpu.make_async_copy(x_hbm, xv, lsem.at[0])
             cg = pltpu.make_async_copy(g_hbm, gv, lsem.at[1])
             ci = pltpu.make_async_copy(ids_hbm, idv, lsem.at[2])
-            cg.start()
-            ci.start()
             for k in range(pos):
                 part = pl.ds(k * batch, batch)
                 pltpu.make_async_copy(x_hbm.at[part], xv.at[part], lsem.at[0]).start()
+            cg.start()
+            ci.start()
 
             def w_copy(kt, group):
                 return pltpu.make_async_copy(
                     w_hbm.at[pl.ds(pl.multiple_of(OWN + y * half, 16), half), pl.ds(pl.multiple_of(kt * TILE, TILE), TILE)],
-                    wv.at[kt], wsem.at[group])
+                    wv.at[kt], wsem.at[group % 3])
 
             def w_start(group):
                 for name in STEPS[group][2]:
@@ -145,7 +145,7 @@
 
             def w_wait(group):
                 some = wv.at[pl.ds(0, len(STEPS[group][2]))]
-                pltpu.make_async_copy(some, some, wsem.at[group]).wait()
+                pltpu.make_async_copy(some, some, wsem.at[group % 3]).wait()
 
             def tile_of(owner, i):
                 if i < unique:
@@ -427,7 +427,7 @@
                 pltpu.VMEM((2, 8, LANES), f32),
                 pltpu.VMEM((2 * tp, 8, LANES), f32),
                 dma((2,)),
-                dma((len(STEPS),)),
+                dma((3,)),
                 dma((4,)),
                 dma,
                 dma((len(Y_GROUPS),)),

time: 26.3 us -> 26.3 us (level)
  no operation moved by 1% of the time
where the time goes in v10:
time: 26.3 us; the launch traced here: 26.2 us
  Pallas kernels  25.6 us (97%)
  between operations  0.64 us (2%)
    pallas_call x1, Pallas kernels, per_device(): pl.pallas_call(kernel, out_shape=pltpu.VMEM((3 * pos, batch), f32), in_sp...  24.9 us
    pallas_call x1, Pallas kernels, per_device(): pl.pallas_call(split, out_shape=[jax.ShapeDtypeStruct((drafts, batch), f3...  0.6 us

profile of v10, /device:TPU:0, one launch (start us, length us, event | category | flops | bytes accessed | tf_op | source)
XLA Modules:
  0.0 26.2 jit_solution(10254788477992619777)
XLA Ops:
  0.6 24.9 %shard_map.67.src = f32[15,16]{1,0:T(8,128)S(1)} custom-call(bf16[80,5120]{1,0:T(8,128)(2,1)} %bitcast.9, s32[4,16]{1,0:T(4,128)} %bitcast.11, bf16[40,128]{1,0:T(8,128)(2,1)} %bitcast.10, bf16[8000,5120]{1,0:T(8,128)(2,1)} %bitcast.4.w_hbm), custom_call_target="tpu_custom_call" | custom-call | tf_op jit(solution)/shard_map/pallas_call | solution.py:409
  25.6 0.6 %shard_map.68 = (f32[4,16]{1,0:T(4,128)}, f32[5,16]{1,0:T(8,128)}, f32[5,16]{1,0:T(8,128)}) custom-call(f32[15,16]{1,0:T(8,128)S(1)} %shard_map.67.src), custom_call_target="tpu_custom_call" | custom-call | tf_op jit(solution)/shard_map/pallas_call | solution.py:448
